TPU v7x, 128 devices: a whole 4x4x4 slice. The times are simulated.
128 devices in a mesh: mpo: 4 (over z), col: 4 (over y), row: 8 (over x, core).
Axes of the slice: x: 4, y: 4, z: 4, core: 2. Of those that a mesh axis runs over, the one named last changes fastest.
Arguments:
- psi_init: float32 [2048, 2, 2, 2048], P('row', None, None, 'col')
- left_env: float32 [2048, 8, 2048], P('row', 'mpo')
- right_env: float32 [2048, 8, 2048], P('col', 'mpo')
- mpo_w12: float32 [8, 8, 2, 2, 2, 2], P('mpo')
Outputs:
- output 1: float32 [4], replicated
- output 2: float32 [4], replicated
- output 3: float32 [2048, 2, 2, 2048], P('row', None, None, 'col')
All inputs are finite; a program needn't handle non-finite values.
Results may differ from a plain program's by a relative error of at most 0.001.
Values sent between devices are 32-bit elements.
A program may use at most 1 GiB of HBM per device.

v0:
```python
import jax
import jax.numpy as jnp
from jax import lax
from jax.sharding import PartitionSpec as P

LANCZOS_STEPS = 4
PREC_HIGH = lax.Precision.HIGHEST
VEC_AXES = ('row', 'col')


def solution(mesh):
    def local_fn(psi_blk, left_blk, right_blk, mpo_blk):
        row_loc = psi_blk.shape[0]
        phys_dim = psi_blk.shape[1]
        col_loc = psi_blk.shape[3]
        phys_sq = phys_dim * phys_dim
        mpo_loc = mpo_blk.shape[0]
        mpo_bond = mpo_blk.shape[1]
        mpo_mat = mpo_blk.reshape(mpo_loc, mpo_bond, phys_sq, phys_sq)
        left_cols = lax.all_to_all(left_blk, 'row', 2, 0, tiled=True)

        def apply_ham(vec_mat):
            vec_full = lax.all_gather(vec_mat, 'row', axis=0, tiled=True)
            t_one = jnp.einsum('alc,asb->lcsb', left_cols, vec_full, precision=PREC_HIGH, preferred_element_type=jnp.float32)
            t_part = jnp.einsum('lcsb,lrst->cbrt', t_one, mpo_mat, precision=PREC_HIGH, preferred_element_type=jnp.float32)
            t_two = lax.psum_scatter(t_part, 'mpo', scatter_dimension=2, tiled=True)
            y_part = jnp.einsum('cbrt,brd->ctd', t_two, right_blk, precision=PREC_HIGH, preferred_element_type=jnp.float32)
            y_cols = lax.psum_scatter(y_part, 'col', scatter_dimension=2, tiled=True)
            return lax.psum(y_cols, 'mpo')

        def global_dot(left_vec, right_vec):
            return lax.psum(jnp.sum(left_vec * right_vec), VEC_AXES)

        vec_cur = psi_blk.reshape(row_loc, phys_sq, col_loc)
        vec_cur = vec_cur / jnp.sqrt(global_dot(vec_cur, vec_cur))
        vec_prev = vec_cur
        beta_prev = jnp.zeros((), jnp.float32)
        alpha_list = []
        beta_list = []
        for step_idx in range(LANCZOS_STEPS):
            h_vec = apply_ham(vec_cur)
            alpha_j = global_dot(vec_cur, h_vec)
            residual = h_vec - alpha_j * vec_cur
            if step_idx > 0:
                residual = residual - beta_prev * vec_prev
            beta_j = jnp.sqrt(global_dot(residual, residual))
            vec_prev = vec_cur
            vec_cur = residual / beta_j
            beta_prev = beta_j
            alpha_list.append(alpha_j)
            beta_list.append(beta_j)
        out_vec = vec_cur.reshape(row_loc, phys_dim, phys_dim, col_loc)
        return jnp.stack(alpha_list), jnp.stack(beta_list), out_vec

    return jax.shard_map(
        local_fn,
        mesh=mesh,
        in_specs=(P('row', None, None, 'col'), P('row', 'mpo', None), P('col', 'mpo', None), P('mpo', None, None, None, None, None)),
        out_specs=(P(), P(), P('row', None, None, 'col')),
        check_vma=False,
    )
```

profile of v0, /device:TPU:1, one launch (start us, length us, event | category | flops | bytes accessed | tf_op | source)
XLA Modules:
  0.0 2626.8 jit_solution(13206041425142451032)
XLA Ops:
  7.2 4.4 multiply_reduce_fusion.8
  11.6 64.4 %psum.91 = f32[]{:T(128)} all-reduce(f32[]{:T(128)} %multiply_reduce_fusion.8), channel_id=1, replica_groups=mesh['mpo'=4,'col'=4,'row'=8] {'row','col'}, use_global_device_ids=true, to_apply=%region_1.0 | all-reduce | flops 1 | bytes 8 | tf_op jit(solution)/shard_map/psum | solution.py:32
  76.7 2.3 broadcast_divide_fusion.4
  79.0 2.5 copy.43
  81.6 9.2 copy.44
  90.8 102.4 %all_to_all.18 = f32[256,2,2048]{0,1,2:T(2,128)S(1)} all-to-all(f32[256,2,2048]{0,1,2:T(2,128)} %copy.44), channel_id=1, replica_groups=mesh['mpo'=4,'col'=4,'row'=8] {'row'}, dimensions={2} | all-to-all | bytes 8388608 | tf_op jit(solution)/shard_map/all_to_all | solution.py:20
  195.5 5.4 copy.46
  200.9 12.9 all-gather.5.cloned.1.call-done
  213.8 32.1 %fusion.28 = f32[2,256,4,512,1]{1,3,0,2,4:T(8,128)} fusion(f32[2048,2,256,1]{2,0,1,3:T(8,128)} %bitcast.117, f32[2048,4,512]{0,2,1:T(8,128)} %all-gather.5.cloned.1.call-done), kind=kOutput, calls=%fused_computation.24 | convolution fusion | flops 25769803776 | bytes 25165824 | tf_op jit(solution)/shard_map/alc,asb->lcsb/dot_general | solution.py:24
  245.8 5.6 copy.73
  251.4 18.4 convolution_bitcast_fusion.3
  269.9 19.5 copy.49
  289.4 148.2 %reduce-scatter.9.cloned.1.call-done = f32[256,512,2,4]{1,0,3,2:T(8,128)} async-done(((f32[256,512,8,4]{1,0,3,2:T(8,128)}), f32[256,512,2,4]{1,0,3,2:T(8,128)}) %reduce-scatter.9.cloned.1.call-update) | async-done | bytes 4194320 | tf_op jit(solution)/shard_map/reduce_scatter | solution.py:26
  437.6 32.1 %fusion.16 = f32[256,4,2048]{0,2,1:T(8,128)} fusion(f32[256,512,2,4]{1,0,3,2:T(8,128)} %reduce-scatter.9.cloned.1.call-done, f32[512,2,2048,1]{2,1,0,3:T(2,128)} %bitcast.125), kind=kOutput, calls=%fused_computation.20 | convolution fusion | flops 25769803776 | bytes 20971520 | tf_op jit(solution)/shard_map/cbrt,brd->ctd/dot_general | solution.py:27
  469.8 80.3 %reduce-scatter.11.cloned.1.call-done = f32[256,4,512]{0,2,1:T(8,128)} async-done(((f32[256,4,2048]{0,2,1:T(8,128)}), f32[256,4,512]{0,2,1:T(8,128)}) %reduce-scatter.11.cloned.1.call-update) | async-done | bytes 2097168 | tf_op jit(solution)/shard_map/reduce_scatter | solution.py:28
  550.3 60.5 %all-reduce.5.cloned.1.call-done = f32[256,4,512]{0,2,1:T(8,128)} async-done(((f32[256,4,512]{0,2,1:T(8,128)}), f32[256,4,512]{0,2,1:T(8,128)}) %all-reduce.5.cloned.1.call-update) | async-done | bytes 2097168 | tf_op jit(solution)/shard_map/psum | solution.py:29
  610.8 2.7 multiply_reduce_fusion.7
  613.5 63.2 %psum.93 = f32[]{:T(128)} all-reduce(f32[]{:T(128)} %multiply_reduce_fusion.7), channel_id=1, replica_groups=mesh['mpo'=4,'col'=4,'row'=8] {'row','col'}, use_global_device_ids=true, to_apply=%region_6.0 | all-reduce | flops 1 | bytes 8 | tf_op jit(solution)/shard_map/psum | solution.py:32
  676.8 3.3 multiply_reduce_fusion.6
  680.1 63.3 %psum.94 = f32[]{:T(128)} all-reduce(f32[]{:T(128)} %multiply_reduce_fusion.6), channel_id=1, replica_groups=mesh['mpo'=4,'col'=4,'row'=8] {'row','col'}, use_global_device_ids=true, to_apply=%region_8.0 | all-reduce | flops 1 | bytes 8 | tf_op jit(solution)/shard_map/psum | solution.py:32
  744.0 3.7 broadcast_divide_fusion.3
  747.9 86.5 %all-gather.7.cloned.1.call-done = f32[2048,4,512]{0,2,1:T(8,128)} async-done(((f32[256,4,512]{0,2,1:T(8,128)}), f32[2048,4,512]{0,2,1:T(8,128)}) %all-gather.7.cloned.1.call-update) | async-done | bytes 16777232 | tf_op jit(solution)/shard_map/all_gather | solution.py:23
  834.3 32.1 %fusion.31 = f32[2,256,4,512,1]{1,3,0,2,4:T(8,128)} fusion(f32[2048,2,256,1]{2,0,1,3:T(8,128)} %bitcast.118, f32[2048,4,512]{0,2,1:T(8,128)} %all-gather.7.cloned.1.call-done), kind=kOutput, calls=%fused_computation.25 | convolution fusion | flops 25769803776 | bytes 25165824 | tf_op jit(solution)/shard_map/alc,asb->lcsb/dot_general | solution.py:24
  866.4 5.6 copy.79
  872.0 18.4 convolution_bitcast_fusion.2
  890.4 19.5 copy.55
  910.0 148.2 %reduce-scatter.13.cloned.1.call-done = f32[256,512,2,4]{1,0,3,2:T(8,128)} async-done(((f32[256,512,8,4]{1,0,3,2:T(8,128)}), f32[256,512,2,4]{1,0,3,2:T(8,128)}) %reduce-scatter.13.cloned.1.call-update) | async-done | bytes 4194320 | tf_op jit(solution)/shard_map/reduce_scatter | solution.py:26
  1058.2 32.1 %fusion.19 = f32[256,4,2048]{0,2,1:T(8,128)} fusion(f32[256,512,2,4]{1,0,3,2:T(8,128)} %reduce-scatter.13.cloned.1.call-done, f32[512,2,2048,1]{2,1,0,3:T(2,128)} %bitcast.126), kind=kOutput, calls=%fused_computation.21 | convolution fusion | flops 25769803776 | bytes 20971520 | tf_op jit(solution)/shard_map/cbrt,brd->ctd/dot_general | solution.py:27
  1090.4 80.2 %reduce-scatter.15.cloned.1.call-done = f32[256,4,512]{0,2,1:T(8,128)} async-done(((f32[256,4,2048]{0,2,1:T(8,128)}), f32[256,4,512]{0,2,1:T(8,128)}) %reduce-scatter.15.cloned.1.call-update) | async-done | bytes 2097168 | tf_op jit(solution)/shard_map/reduce_scatter | solution.py:28
  1170.8 60.6 %all-reduce.7.cloned.1.call-done = f32[256,4,512]{0,2,1:T(8,128)} async-done(((f32[256,4,512]{0,2,1:T(8,128)}), f32[256,4,512]{0,2,1:T(8,128)}) %all-reduce.7.cloned.1.call-update) | async-done | bytes 2097168 | tf_op jit(solution)/shard_map/psum | solution.py:29
  1231.5 3.4 multiply_reduce_fusion.5
  1234.8 63.3 %psum.96 = f32[]{:T(128)} all-reduce(f32[]{:T(128)} %multiply_reduce_fusion.5), channel_id=1, replica_groups=mesh['mpo'=4,'col'=4,'row'=8] {'row','col'}, use_global_device_ids=true, to_apply=%region_13.0 | all-reduce | flops 1 | bytes 8 | tf_op jit(solution)/shard_map/psum | solution.py:32
  1298.2 5.5 multiply_reduce_fusion.4
  1303.7 63.3 %psum.97 = f32[]{:T(128)} all-reduce(f32[]{:T(128)} %get-tuple-element.19), channel_id=1, replica_groups=mesh['mpo'=4,'col'=4,'row'=8] {'row','col'}, use_global_device_ids=true, to_apply=%region_15.0 | all-reduce | flops 1 | bytes 8 | tf_op jit(solution)/shard_map/psum | solution.py:32
  1367.7 3.1 broadcast_divide_fusion.2
  1370.8 86.5 %all-gather.9.cloned.1.call-done = f32[2048,4,512]{0,2,1:T(8,128)} async-done(((f32[256,4,512]{0,2,1:T(8,128)}), f32[2048,4,512]{0,2,1:T(8,128)}) %all-gather.9.cloned.1.call-update) | async-done | bytes 16777232 | tf_op jit(solution)/shard_map/all_gather | solution.py:23
  1457.3 32.1 %fusion.34 = f32[2,256,4,512,1]{1,3,0,2,4:T(8,128)} fusion(f32[2048,2,256,1]{2,0,1,3:T(8,128)} %bitcast.119, f32[2048,4,512]{0,2,1:T(8,128)} %all-gather.9.cloned.1.call-done), kind=kOutput, calls=%fused_computation.26 | convolution fusion | flops 25769803776 | bytes 25165824 | tf_op jit(solution)/shard_map/alc,asb->lcsb/dot_general | solution.py:24
  1489.4 5.6 copy.85
  1494.9 18.4 convolution_bitcast_fusion.1
  1513.4 19.5 copy.61
  1533.0 148.2 %reduce-scatter.17.cloned.1.call-done = f32[256,512,2,4]{1,0,3,2:T(8,128)} async-done(((f32[256,512,8,4]{1,0,3,2:T(8,128)}), f32[256,512,2,4]{1,0,3,2:T(8,128)}) %reduce-scatter.17.cloned.1.call-update) | async-done | bytes 4194320 | tf_op jit(solution)/shard_map/reduce_scatter | solution.py:26
  1681.2 32.1 %fusion.22 = f32[256,4,2048]{0,2,1:T(8,128)} fusion(f32[256,512,2,4]{1,0,3,2:T(8,128)} %reduce-scatter.17.cloned.1.call-done, f32[512,2,2048,1]{2,1,0,3:T(2,128)} %bitcast.127), kind=kOutput, calls=%fused_computation.22 | convolution fusion | flops 25769803776 | bytes 20971520 | tf_op jit(solution)/shard_map/cbrt,brd->ctd/dot_general | solution.py:27
  1713.4 80.2 %reduce-scatter.19.cloned.1.call-done = f32[256,4,512]{0,2,1:T(8,128)} async-done(((f32[256,4,2048]{0,2,1:T(8,128)}), f32[256,4,512]{0,2,1:T(8,128)}) %reduce-scatter.19.cloned.1.call-update) | async-done | bytes 2097168 | tf_op jit(solution)/shard_map/reduce_scatter | solution.py:28
  1793.8 60.5 %all-reduce.9.cloned.1.call-done = f32[256,4,512]{0,2,1:T(8,128)} async-done(((f32[256,4,512]{0,2,1:T(8,128)}), f32[256,4,512]{0,2,1:T(8,128)}) %all-reduce.9.cloned.1.call-update) | async-done | bytes 2097168 | tf_op jit(solution)/shard_map/psum | solution.py:29
  1854.3 2.7 multiply_reduce_fusion.3
  1857.1 63.3 %psum.99 = f32[]{:T(128)} all-reduce(f32[]{:T(128)} %multiply_reduce_fusion.3), channel_id=1, replica_groups=mesh['mpo'=4,'col'=4,'row'=8] {'row','col'}, use_global_device_ids=true, to_apply=%region_20.0 | all-reduce | flops 1 | bytes 8 | tf_op jit(solution)/shard_map/psum | solution.py:32
  1920.4 5.2 multiply_reduce_fusion.2
  1925.6 63.3 %psum.100 = f32[]{:T(128)} all-reduce(f32[]{:T(128)} %get-tuple-element.17), channel_id=1, replica_groups=mesh['mpo'=4,'col'=4,'row'=8] {'row','col'}, use_global_device_ids=true, to_apply=%region_22.0 | all-reduce | flops 1 | bytes 8 | tf_op jit(solution)/shard_map/psum | solution.py:32
  1989.6 3.1 broadcast_divide_fusion.1
  1992.8 86.5 %all-gather.11.cloned.1.call-done = f32[2048,4,512]{0,2,1:T(8,128)} async-done(((f32[256,4,512]{0,2,1:T(8,128)}), f32[2048,4,512]{0,2,1:T(8,128)}) %all-gather.11.cloned.1.call-update) | async-done | bytes 16777232 | tf_op jit(solution)/shard_map/all_gather | solution.py:23
  2079.2 32.1 %fusion.37 = f32[2,256,4,512,1]{1,3,0,2,4:T(8,128)} fusion(f32[2048,2,256,1]{2,0,1,3:T(8,128)} %bitcast.120, f32[2048,4,512]{0,2,1:T(8,128)} %all-gather.11.cloned.1.call-done), kind=kOutput, calls=%fused_computation.27 | convolution fusion | flops 25769803776 | bytes 25165824 | tf_op jit(solution)/shard_map/alc,asb->lcsb/dot_general | solution.py:24
  2111.3 5.6 copy.91
  2116.9 18.4 convolution_bitcast_fusion
  2135.3 19.3 copy.67
  2154.7 148.2 %reduce-scatter.21.cloned.1.call-done = f32[256,512,2,4]{1,0,3,2:T(8,128)} async-done(((f32[256,512,8,4]{1,0,3,2:T(8,128)}), f32[256,512,2,4]{1,0,3,2:T(8,128)}) %reduce-scatter.21.cloned.1.call-update) | async-done | bytes 4194320 | tf_op jit(solution)/shard_map/reduce_scatter | solution.py:26
  2302.9 32.1 %fusion.25 = f32[256,4,2048]{0,2,1:T(8,128)} fusion(f32[256,512,2,4]{1,0,3,2:T(8,128)} %reduce-scatter.21.cloned.1.call-done, f32[512,2,2048,1]{2,1,0,3:T(2,128)} %bitcast.128), kind=kOutput, calls=%fused_computation.23 | convolution fusion | flops 25769803776 | bytes 20971520 | tf_op jit(solution)/shard_map/cbrt,brd->ctd/dot_general | solution.py:27
  2335.1 80.3 %reduce-scatter.23.cloned.1.call-done = f32[256,4,512]{0,2,1:T(8,128)} async-done(((f32[256,4,2048]{0,2,1:T(8,128)}), f32[256,4,512]{0,2,1:T(8,128)}) %reduce-scatter.23.cloned.1.call-update) | async-done | bytes 2097168 | tf_op jit(solution)/shard_map/reduce_scatter | solution.py:28
  2415.4 60.7 %all-reduce.11.cloned.1.call-done = f32[256,4,512]{0,2,1:T(8,128)} async-done(((f32[256,4,512]{0,2,1:T(8,128)}), f32[256,4,512]{0,2,1:T(8,128)}) %all-reduce.11.cloned.1.call-update) | async-done | bytes 2097168 | tf_op jit(solution)/shard_map/psum | solution.py:29
  2476.1 3.4 multiply_reduce_fusion.1
  2479.5 63.3 %psum.102 = f32[]{:T(128)} all-reduce(f32[]{:T(128)} %multiply_reduce_fusion.1), channel_id=1, replica_groups=mesh['mpo'=4,'col'=4,'row'=8] {'row','col'}, use_global_device_ids=true, to_apply=%region_27.0 | all-reduce | flops 1 | bytes 8 | tf_op jit(solution)/shard_map/psum | solution.py:32
  2542.8 5.3 multiply_reduce_fusion
  2548.1 63.3 %psum.103 = f32[]{:T(128)} all-reduce(f32[]{:T(128)} %get-tuple-element.15), channel_id=1, replica_groups=mesh['mpo'=4,'col'=4,'row'=8] {'row','col'}, use_global_device_ids=true, to_apply=%region_29.0 | all-reduce | flops 1 | bytes 8 | tf_op jit(solution)/shard_map/psum | solution.py:32
  2613.8 2.3 copy.71
  2616.8 3.1 pad_maximum_fusion
  (41 shorter events, 6.1 us)
Async XLA Ops:
  7.2 206.6 %all-gather.5.cloned.1.call-start = ((), (), s32[]{:S(2)}) async-start(), calls=%async_computation.9 | async-start | bytes 18874368 | tf_op jit(solution)/shard_map/all_gather | solution.py:23
  81.5 356.1 %reduce-scatter.9.cloned.1.call-start = ((), (), s32[]{:S(2)}) async-start(), calls=%async_computation.10 | async-start | bytes 20971520 | tf_op jit(solution)/shard_map/reduce_scatter | solution.py:26
  245.8 5.6 copy-start.2
  289.4 260.7 %reduce-scatter.11.cloned.1.call-start = ((), (), s32[]{:S(2)}) async-start(), calls=%async_computation.11 | async-start | bytes 10485760 | tf_op jit(solution)/shard_map/reduce_scatter | solution.py:28
  469.7 141.1 %copy-start = (f32[256,2,2,512]{0,3,2,1:T(8,128)S(1)}, f32[256,2,2,512]{0,3,2,1:T(8,128)}, u32[]{:S(2)}) copy-start(f32[256,2,2,512]{0,3,2,1:T(8,128)} %copy.43) | copy-start | bytes 6291460
  469.8 141.0 %all-reduce.5.cloned.1.call-start = ((), (), s32[]{:S(2)}) async-start(), calls=%async_computation.12 | async-start | bytes 4194304 | tf_op jit(solution)/shard_map/psum | solution.py:29
  550.1 284.2 %all-gather.7.cloned.1.call-start = ((), (), s32[]{:S(2)}) async-start(), calls=%async_computation.13 | async-start | bytes 18874368 | tf_op jit(solution)/shard_map/all_gather | solution.py:23
  747.8 310.4 %reduce-scatter.13.cloned.1.call-start = ((), (), s32[]{:S(2)}) async-start(), calls=%async_computation.14 | async-start | bytes 20971520 | tf_op jit(solution)/shard_map/reduce_scatter | solution.py:26
  909.9 260.7 %reduce-scatter.15.cloned.1.call-start = ((), (), s32[]{:S(2)}) async-start(), calls=%async_computation.15 | async-start | bytes 10485760 | tf_op jit(solution)/shard_map/reduce_scatter | solution.py:28
  1090.3 141.2 %all-reduce.7.cloned.1.call-start = ((), (), s32[]{:S(2)}) async-start(), calls=%async_computation.16 | async-start | bytes 4194304 | tf_op jit(solution)/shard_map/psum | solution.py:29
  1170.6 286.7 %all-gather.9.cloned.1.call-start = ((), (), s32[]{:S(2)}) async-start(), calls=%async_computation.17 | async-start | bytes 18874368 | tf_op jit(solution)/shard_map/all_gather | solution.py:23
  1370.8 310.4 %reduce-scatter.17.cloned.1.call-start = ((), (), s32[]{:S(2)}) async-start(), calls=%async_computation.18 | async-start | bytes 20971520 | tf_op jit(solution)/shard_map/reduce_scatter | solution.py:26
  1532.9 260.7 %reduce-scatter.19.cloned.1.call-start = ((), (), s32[]{:S(2)}) async-start(), calls=%async_computation.19 | async-start | bytes 10485760 | tf_op jit(solution)/shard_map/reduce_scatter | solution.py:28
  1713.3 141.1 %copy-start.1 = (f32[256,4,512]{0,2,1:T(8,128)S(1)}, f32[256,4,512]{0,2,1:T(8,128)}, u32[]{:S(2)}) copy-start(f32[256,4,512]{0,2,1:T(8,128)} %get-tuple-element.20) | copy-start | bytes 6291460
  1713.3 141.0 %all-reduce.9.cloned.1.call-start = ((), (), s32[]{:S(2)}) async-start(), calls=%async_computation.20 | async-start | bytes 4194304 | tf_op jit(solution)/shard_map/psum | solution.py:29
  1793.6 285.6 %all-gather.11.cloned.1.call-start = ((), (), s32[]{:S(2)}) async-start(), calls=%async_computation.21 | async-start | bytes 18874368 | tf_op jit(solution)/shard_map/all_gather | solution.py:23
  1992.7 310.2 %reduce-scatter.21.cloned.1.call-start = ((), (), s32[]{:S(2)}) async-start(), calls=%async_computation.22 | async-start | bytes 20971520 | tf_op jit(solution)/shard_map/reduce_scatter | solution.py:26
  2154.7 260.7 %reduce-scatter.23.cloned.1.call-start = ((), (), s32[]{:S(2)}) async-start(), calls=%async_computation.23 | async-start | bytes 10485760 | tf_op jit(solution)/shard_map/reduce_scatter | solution.py:28
  2335.0 141.0 %all-reduce.11.cloned.1.call-start = ((), (), s32[]{:S(2)}) async-start(), calls=%async_computation.24 | async-start | bytes 4194304 | tf_op jit(solution)/shard_map/psum | solution.py:29
Sparse Core Ops, SparseCore 0:
  81.7 132.0 all-gather.4
  289.5 148.0 reduce-scatter.8
  469.9 80.1 reduce-scatter.10
  552.3 58.4 all-reduce.4
  747.9 86.3 all-gather.6
  910.0 148.1 reduce-scatter.12
  1090.4 80.1 reduce-scatter.14
  1173.0 58.4 all-reduce.6
  1370.9 86.3 all-gather.8
  1533.0 148.1 reduce-scatter.16
  1713.4 80.1 reduce-scatter.18
  1795.8 58.4 all-reduce.8
  1992.8 86.3 all-gather.10
  2154.8 148.0 reduce-scatter.20
  2335.2 80.1 reduce-scatter.22
  2417.6 58.4 all-reduce.10
where the time goes:
time: 2640 us; the launch traced here: 2630 us
  waiting for transfers between devices  1430 us (54%)
  blocking collectives  673 us (25%)
  matrix products  330 us (12%)
  local copies, waits for them, and re-layouts  122 us (5%)
  other arithmetic  53.6 us (2%)
    reduce_scatter x4, waiting for transfers between devices, apply_ham(): t_two = lax.psum_scatter(t_part, 'mpo', scatter_dimension=2, tiled=True)  593 us
    psum x9, blocking collectives, global_dot(): return lax.psum(jnp.sum(left_vec * right_vec), VEC_AXES)  571 us
    reduce_scatter x4, waiting for transfers between devices, apply_ham(): y_cols = lax.psum_scatter(y_part, 'col', scatter_dimension=2, tiled=True)  321 us
    all_gather x4, waiting for transfers between devices, apply_ham(): vec_full = lax.all_gather(vec_mat, 'row', axis=0, tiled=True)  272 us
    psum x4, waiting for transfers between devices, apply_ham(): return lax.psum(y_cols, 'mpo')  242 us
    dot_general x4, matrix products, apply_ham(): jnp.einsum('cbrt,brd->ctd', t_two, right_blk, precision=PREC_HIGH, prefer...  128 us
    dot_general x4, matrix products, apply_ham(): jnp.einsum('alc,asb->lcsb', left_cols, vec_full, precision=PREC_HIGH, pre...  128 us
    all_to_all x1, blocking collectives, local_fn(): left_cols = lax.all_to_all(left_blk, 'row', 2, 0, tiled=True)  102 us
  transfers between devices with their start and end apart: 16, of which 16 were waited for; matrix products, arithmetic and copies ran while one was open for 1% of the time, Pallas kernels for 0%

commit v1 on v0

v1 whole, which is shorter than its diff:
```python
import jax
import jax.numpy as jnp
from jax import lax
from jax.experimental import pallas as pl
from jax.experimental.pallas import tpu as pltpu
from jax.sharding import PartitionSpec as P

STEPS = 4
F32 = jnp.float32
MIB = 2**20


(FAR_P, FAR_M, NEAR_P, NEAR_M, LO, HI, OWN_P, OWN_M, OWN_D, ALT_P, ALT_M, ALT_D, FWD_P, DP_O, DM_O, DP_A, DM_A,
 FWD_M, DF_O, DF_A) = range(20)
N_COPY, N_REDUCE = 20, 5


HALVES = (0, 1)
OTHERS = (1, 2, 3)
FAR_FIRST = (2, 1, 3)
CHIPS, CORES, ROWS = 4, 2, 8


def dot_hi(a, b):
    return lax.dot_general(a, b, (((1,), (0,)), ((), ())), precision=lax.Precision.HIGHEST, preferred_element_type=F32)


def hi_of(z):
    return lax.div(z, 2)


def lo_of(z):
    return lax.rem(lax.div(z + 1, 2), 2)


def remote(src, dst, send, recv, device):
    return pltpu.make_async_remote_copy(src_ref=src, dst_ref=dst, send_sem=send, recv_sem=recv, device_id=device,
                                        device_id_type=pl.DeviceIdType.MESH)


def signal(sem, device):
    pl.semaphore_signal(sem, inc=1, device_id=device, device_id_type=pl.DeviceIdType.MESH)


def block(start, n):
    return pl.ds(pl.multiple_of(start, n), n)


class Around:
    def __init__(self):
        self.row, self.col, self.mpo = (lax.axis_index(a) for a in ('row', 'col', 'mpo'))
        self.x, self.c = lax.div(self.row, CORES), lax.rem(self.row, CORES)
        self.hi, self.lo = hi_of(self.mpo), lo_of(self.mpo)
        (self.xp, self.x2, self.xm), (self.yp, self.y2, self.ym) = (
            [lax.rem(v + d, CHIPS) for d in OTHERS] for v in (self.x, self.col))
        self.other = 1 - self.c
        self.to_xp, self.to_xm = ({'row': v * CORES + self.c} for v in (self.xp, self.xm))
        self.to_core = {'row': self.x * CORES + self.other}
        self.to_yp, self.to_ym = {'col': self.yp}, {'col': self.ym}
        self.to_lo = {'mpo': self.mpo + 1 - CORES * lax.rem(self.mpo, CORES)}
        self.to_hi = {'mpo': CHIPS - 1 - self.mpo}

    def turn(self, **steps):
        size = {'row': ROWS, 'col': CHIPS, 'mpo': CHIPS}
        return {a: lax.rem(getattr(self, a) + d, size[a]) for a, d in steps.items()}


def got(ref, send, recv, device):
    remote(ref, ref, send, recv, device).wait_recv()


class Ring:
    def __init__(self, me, at, first, send, recv):
        x, c, o = me.x, me.c, me.other
        whole = [(at(me.xm, c), me.to_core), (at(me.xp, c), me.to_core)]
        halves = [at(me.x2, c, h) for h in HALVES]
        self.moves = [(first, at(x, c), d) for d in (me.to_xp, me.to_xm, me.to_core)]
        self.moves += [(r, r, d) for r, d in (
            (at(me.xm, c, 0), me.to_xp), (at(me.xp, c, 1), me.to_xm), *whole, *((h, me.to_core) for h in halves))]
        self.lands = [at(me.xm, c), at(me.xp, c), at(x, o), *halves, at(me.xm, o), at(me.xp, o),
                      *(at(me.x2, o, h) for h in HALVES)]
        self.send, self.recv, self.device = send, recv, me.to_core

    def copy(self, k):
        return remote(*self.moves[k][:2], self.send.at[k], self.recv.at[k], self.moves[k][-1])

    def start(self, *ks):
        for k in ks:
            self.copy(k).start()

    def got(self, *ks):
        for k in ks:
            got(self.lands[k], self.send.at[k], self.recv.at[k], self.device)


(R_P, R_M, R_CORE, R_FWD_P, R_FWD_M, R_CORE_M, R_CORE_P, R_CORE_F0, R_CORE_F1) = range(9)


def setup_kernel(psi, left, right, w, hg, lg, rg, wg, st_psi, st_r, psi_s, psi_r, l1_s, l1_r, ly_s, ly_r, rz_s, rz_r,
                 rx_s, rx_r, rd_s, rd_r, w_s, w_r, loc):
    me = Around()
    row, col, mpo, c, o = me.row, me.col, me.mpo, me.c, me.other
    aw, bw, nb = psi.shape[0], psi.shape[-1], right.shape[-1]
    ah, bh, qa = aw // 2, bw // 2, aw // CHIPS
    half, zc, xc = nb // 2, nb // CHIPS, nb // (2 * ROWS)
    here = me.to_core
    plane = [(dr, dz) for dz in (2, 1, 3, 0) for dr in (4, 5, 2, 3, 6, 7, 1, 0)]

    bar = pltpu.get_barrier_semaphore()
    for dr, dz in plane[:-1]:
        signal(bar, me.turn(row=dr, mpo=dz))
    signal(bar, me.to_yp)
    signal(bar, me.to_ym)
    pl.semaphore_wait(bar, len(plane) + 1)

    for dr, dz in plane:
        to = me.turn(row=dr, mpo=dz)
        for l in HALVES:
            src = left.at[block(col * qa, qa), l, block(to['row'] * aw + hi_of(to['mpo']) * ah, ah)]
            dst = lg.at[mpo * 2 + l, row, col]
            if dr or dz:
                remote(src, dst, l1_s, l1_r, to).start()
            else:
                pltpu.make_async_copy(src, dst, l1_r).start()

    def r_rows(q, rl):
        return block((q * 2 + rl) * bh, bh)

    def r_src(z, rl, start, n):
        return right.at[block(lo_of(z) * bh, bh), rl, block(start, n)]

    def x_cols(x, core):
        return half + (x * CORES + core) * xc

    def r_part(g):
        return (x_cols(me.x, c), xc) if g == 0 else (c * zc, zc)

    def r_copies(g):
        for dz in FAR_FIRST:
            to = me.turn(mpo=dz)
            for rl in HALVES:
                sems = rz_s.at[dz - 1, rl, g], rz_r.at[dz - 1, rl, g]
                yield remote(r_src(to['mpo'], rl, *r_part(g)), rg.at[r_rows(CHIPS - dz, rl), block(*r_part(g))], *sems, to)

    def r_got(g):
        for dz in FAR_FIRST:
            for rl in HALVES:
                got(rg.at[r_rows(CHIPS - dz, rl), block(*r_part(g))], rz_s.at[dz - 1, rl, g], rz_r.at[dz - 1, rl, g], here)

    def w_copy(dz):
        return remote(w, wg.at[mpo], w_s.at[dz - 1], w_r.at[dz - 1], me.turn(mpo=dz))

    for copy in r_copies(0):
        copy.start()

    def psi_at(t):
        def at(x, core, h=None):
            start = (x * CORES + core) * aw
            return hg.at[t, block(start, aw) if h is None else block(start + h * ah, ah), :]
        return at

    def psi_src(t):
        return psi.at[:, t // 2, t % 2, block(me.lo * bh, bh)]

    slices = range(CHIPS)
    psi_rings = [Ring(me, psi_at(t), psi_src(t), psi_s.at[t], psi_r.at[t]) for t in slices]
    for ring in psi_rings:
        ring.start(R_P, R_M, R_CORE)
    for copy in r_copies(1):
        copy.start()
    for dz in OTHERS:
        w_copy(dz).start()

    own = [(w, wg.at[mpo], None)]
    own += [(psi_src(t), psi_at(t)(me.x, c), st_psi.at[t]) for t in slices]
    own += [(r_src(mpo, rl, 0, nb), rg.at[r_rows(0, rl), :], st_r.at[rl]) for rl in HALVES]
    for i, (src, dst, via) in enumerate(own):
        pltpu.make_async_copy(src, dst if via is None else via, loc.at[i]).start()
    for i, (src, dst, via) in enumerate(own):
        if via is not None:
            pltpu.make_async_copy(src, via, loc.at[i]).wait()
            pltpu.make_async_copy(via, dst, loc.at[i]).start()

    ls = range(2 * CHIPS)

    def l_at(y, h=None):
        return lg.at[0:len(ls) if h is None else CHIPS, :, y] if not h else lg.at[CHIPS:len(ls), :, y]

    ly_moves = [(l_at(col), me.to_yp), (l_at(col), me.to_ym), (l_at(me.ym, 0), me.to_yp), (l_at(me.yp, 1), me.to_ym)]
    ly = [remote(ref, ref, ly_s.at[k], ly_r.at[k], d) for k, (ref, d) in enumerate(ly_moves)]
    ly_lands = [l_at(me.ym), l_at(me.yp), l_at(me.y2, 0), l_at(me.y2, 1)]

    def ly_got(k):
        got(ly_lands[k], ly_s.at[k], ly_r.at[k], here)

    got(l_at(col), l1_s, l1_r, here)
    ly[0].start()
    ly[1].start()

    def rx_at(x, core, h=None):
        n = 6 * bh
        rows = pl.ds(2 * bh, n) if h is None else pl.ds(2 * bh + h * n // 2, n // 2)
        return rg.at[rows, block(x_cols(x, core), xc)]

    r_got(0)
    rx = Ring(me, rx_at, rx_at(me.x, c), rx_s, rx_r)
    rx.start(R_P, R_M, R_CORE)
    for ring in psi_rings:
        ring.got(R_P)
        ring.start(R_FWD_P, R_CORE_M)
        ring.got(R_M)
        ring.start(R_FWD_M, R_CORE_P)
    r_got(1)

    def rd_at(core):
        return rg.at[pl.ds(2 * bh, 6 * bh), block(core * zc, zc)]

    rd = remote(rd_at(c), rd_at(c), rd_s, rd_r, here)
    rd.start()
    rx.got(R_P)
    rx.start(R_FWD_P, R_CORE_M)
    rx.got(R_M)
    rx.start(R_FWD_M, R_CORE_P)
    for k in HALVES:
        ly_got(k)
        ly[2 + k].start()
    for ring in (*psi_rings, rx):
        ring.got(R_FWD_P)
        ring.start(R_CORE_F0)
        ring.got(R_FWD_M)
        ring.start(R_CORE_F1)
    for k in HALVES:
        ly_got(2 + k)

    for ring in (*psi_rings, rx):
        ring.got(R_CORE, R_CORE_M, R_CORE_P, R_CORE_F0, R_CORE_F1)
    got(rd_at(o), rd_s, rd_r, here)
    for dz in OTHERS:
        got(wg.at[lax.rem(mpo + CHIPS - dz, CHIPS)], w_s.at[dz - 1], w_r.at[dz - 1], here)
    for i, (src, dst, via) in enumerate(own):
        pltpu.make_async_copy(src if via is None else via, dst, loc.at[i]).wait()
    for ring in (*psi_rings, rx):
        for k in range(len(ring.moves)):
            ring.copy(k).wait_send()
    for copy in (*ly, *r_copies(0), *r_copies(1), *(w_copy(dz) for dz in OTHERS), rd):
        copy.wait_send()
    for ref in (lg.at[0:len(ls) - 1, :, 0], lg.at[0, 0:ROWS - 2, 0]):
        remote(ref, ref, l1_s, l1_r, here).wait_send()


def lanczos(hg, lt, rg, wg, out, ab, R, L, G, U, W3, T1, T2, TP, PY, RF, RN, RZ, V, AL, BE, BP, INV, ARS, AR1,
                 AR2, load, send, recv, ar1_s, ar1_r, ar2_s, ar2_r, credit, z_s, z_r, o_s):
    me = Around()
    row, col, mpo, x, c, hi, lo = me.row, me.col, me.mpo, me.x, me.c, me.hi, me.lo
    n_s, nb, bh = G.shape
    aw, bw = nb // ROWS, CORES * bh
    ah = aw // 2
    n_r, alt, o, last = 2 * CHIPS, 1 - hi, me.other, n_s - 1
    here, me2 = me.to_core, col * CHIPS + mpo
    slices, tile = range(n_s), AL.shape[0]
    others = [(dc, dz) for dc in range(CHIPS) for dz in range(CHIPS) if dc or dz]
    peers = [me.turn(row=d) for d in range(1, ROWS)] + [me.turn(col=dc, mpo=dz) for dc, dz in others]

    bar = pltpu.get_barrier_semaphore()
    for peer in peers:
        signal(bar, peer)

    def l_load(i, k):
        j = i % n_s
        return pltpu.make_async_copy(lt.at[pl.ds(i * ah, ah), k * bw:(k + 1) * bw], PY.at[j, k], load.at[j, k])

    n_k = range(nb // bw)
    for i in slices:
        for k in n_k:
            l_load(i, k).start()
    load_g, load_r = (pltpu.make_async_copy(src, dst, load.at[n_s, i]) for i, (src, dst) in enumerate(((hg, G), (rg, R))))
    load_g.start()
    load_r.start()

    U[...] = jnp.concatenate([wg[z][:, :U.shape[1] // CHIPS] for z in range(CHIPS)], axis=1)
    lane, sub = (lax.broadcasted_iota(jnp.int32, (tile, U.shape[1]), i) for i in (1, 0))
    diagonal = jnp.where(lax.rem(lane, tile) == sub, 1.0, 0.0)
    for t in slices:
        for r in range(0, n_r, 2):
            rows = [U[pl.ds(t * n_r + lax.rem(r + i + 2 * mpo, n_r), 1), :] * diagonal for i in HALVES]
            at = (t * n_r + r) * tile
            W3[at:at + 2 * tile] = jnp.concatenate(rows)
    for ref in (T2, TP, V, BP):
        ref[...] = jnp.zeros_like(ref)
    for i in range(n_r):
        for k in n_k:
            l_load(i, k).wait()
            L[i * ah:(i + 1) * ah, k * bw:(k + 1) * bw] = PY[i % n_s, k]
            if i < n_s:
                l_load(i + n_s, k).start()
    pl.semaphore_wait(bar, len(peers))
    load_g.wait()

    def rows_of(xx, cc, hh):
        return block((xx * CORES + cc) * aw + hh * ah, ah)

    own_rows = rows_of(x, c, hi)
    low, high = slice(0, bh), slice(bh, bw)

    def ends(k, t):
        def g_at(xx, cc, hh):
            return G.at[t, rows_of(xx, cc, hh), :]

        xp, xm, x2 = me.xp, me.xm, me.x2
        via = {
            HI: ((x, c, hi), (x, c, alt), me.to_hi),
            OWN_P: ((x, c, hi), (xm, c, hi), me.to_xp),
            OWN_M: ((x, c, hi), (xp, c, hi), me.to_xm),
            ALT_P: ((x, c, alt), (xm, c, alt), me.to_xp),
            ALT_M: ((x, c, alt), (xp, c, alt), me.to_xm),
            FWD_P: ((xm, c, hi), (x2, c, hi), me.to_xp),
            FWD_M: ((xp, c, alt), (x2, c, alt), me.to_xm),
        }
        for kind, xx, hh in ((OWN_D, x, hi), (ALT_D, x, alt), (DP_O, xp, hi), (DM_O, xm, hi), (DP_A, xp, alt),
                             (DM_A, xm, alt), (DF_O, x2, hi), (DF_A, x2, alt)):
            via[kind] = ((xx, c, hh), (xx, o, hh), me.to_core)
        if k in via:
            src, land, to = via[k]
            return g_at(*src), g_at(*src), g_at(*land), to
        far, plus, minus, own = (PY.at[t, i] for i in range(4))
        src, dst, to = {
            FAR_P: (far.at[:, low], RF.at[t, 0], me.to_yp),
            FAR_M: (far.at[:, high], RF.at[t, 1], me.to_ym),
            NEAR_P: (plus, RN.at[t, 0], me.to_yp),
            NEAR_M: (minus, RN.at[t, 1], me.to_ym),
            LO: (own.at[:, block((1 - lo) * bh, bh)], RZ.at[t], me.to_lo),
        }[k]
        return src, dst, dst, to

    def copy(k, t):
        src, dst, _, to = ends(k, t)
        return remote(src, dst, send.at[t, k], recv.at[t, k], to)

    def start(t, *kinds):
        for k in kinds:
            copy(k, t).start()

    def arrived(t, *kinds):
        for k in kinds:
            got(ends(k, t)[2], send.at[t, k], recv.at[t, k], here)

    def e1(t):
        start(t, FAR_P, FAR_M)

    def e2(t):
        arrived(t, FAR_P, FAR_M)
        PY[t, 1, :, low] += RF[t, 0]
        PY[t, 2, :, high] += RF[t, 1]
        start(t, NEAR_P, NEAR_M)

    def e3(t):
        arrived(t, NEAR_P, NEAR_M)
        PY[t, 3] += RN[t, 0] + RN[t, 1]
        start(t, LO)

    def e4(t):
        arrived(t, LO)
        G[t, own_rows, :] = PY[t, 3, :, block(lo * bh, bh)] + RZ[t]

    def g4(t):
        start(t, HI, OWN_P, OWN_M, OWN_D)

    def g5a(t):
        arrived(t, HI)
        start(t, ALT_P, ALT_M, ALT_D)

    def g5b(t):
        arrived(t, OWN_P)
        start(t, FWD_P, DM_O)
        arrived(t, OWN_M)
        start(t, DP_O)

    def g6a(t):
        arrived(t, ALT_M)
        start(t, FWD_M, DP_A)
        arrived(t, ALT_P)
        start(t, DM_A)

    def g6b(t):
        arrived(t, FWD_P)
        start(t, DF_O)

    def g7(t):
        arrived(t, FWD_M)
        start(t, DF_A)

    def ar_pair(k, stage):
        slots, s_sem, r_sem = ((AR1, ar1_s, ar1_r), (AR2, ar2_s, ar2_r))[stage]
        n = len(peers) - len(others) if stage == 0 else len(others)
        ref = slots.at[k, 0:n]
        return remote(ref, ref, s_sem.at[k], r_sem.at[k], here)

    def ar_send(k, stage, part):
        slots, s_sem, r_sem, mine = ((AR1, ar1_s, ar1_r, row), (AR2, ar2_s, ar2_r, me2))[stage]
        ARS[k, stage] = part
        slots[k, mine] = part
        first = len(peers) - len(others)
        for peer in (peers[first:] if stage else peers[:first]):
            remote(ARS.at[k, stage], slots.at[k, mine], s_sem.at[k], r_sem.at[k], peer).start()

    def ar_sum(k, stage):
        ar_pair(k, stage).wait_recv()
        slots = (AR1, AR2)[stage]
        return sum((slots[k, i] for i in range(1, slots.shape[1])), slots[k, 0])

    def ar_end(k):
        tot = jnp.sum(ar_sum(k, 1))
        for stage in HALVES:
            ar_pair(k, stage).wait_send()
        return tot

    def fold(v):
        v = jnp.sum(v.reshape(ah // tile, tile, bh), axis=0)
        n = ARS.shape[-1]
        return sum((v[:, i:i + n] for i in range(n, bh, n)), v[:, :n])

    def a1(j):
        p = lax.rem(j, 2)
        parts = [fold(V[p, t] * G[t, own_rows, :]) for t in slices]
        ar_send(0, 0, sum(parts[1:], parts[0]))

    def a2():
        ar_send(0, 1, ar_sum(0, 0))

    def a3(j):
        p = lax.rem(j, 2)
        AL[...] = jnp.full(AL.shape, ar_end(0), F32)
        al, bp, parts = AL[0:1, :], BP[0:1, :], []
        for t in slices:
            w = G[t, own_rows, :] - al * V[p, t] - bp * V[1 - p, t]
            V[1 - p, t] = w
            parts.append(fold(w * w))
        ar_send(1, 0, sum(parts[1:], parts[0]))

    def b2():
        ar_send(1, 1, ar_sum(1, 0))

    def b3(j):
        p = lax.rem(j, 2)
        BE[...] = jnp.sqrt(jnp.full(BE.shape, ar_end(1), F32))
        INV[...] = 1.0 / BE[...]
        for t in slices:
            V[1 - p, t] = V[1 - p, t] / BE[0:1, :]
        for i, ref in enumerate((AL, BE)):
            ab[i, j] = ref[:, :ab.shape[-1]]

    @pl.loop(0, STEPS)
    def _(j):
        later, more = j > 0, j < STEPS - 1

        def t1_tick(s, xx, first=False):
            ks = block(xx * CORES * aw, CORES * aw)
            n = n_r * ah // 2
            for m in HALVES:
                ms = slice(m * n, (m + 1) * n)
                d = dot_hi(L[ms, ks], G[s, ks, :])
                if first:
                    T1[s, ms] = d
                else:
                    T1[s, ms] += d

        @pl.loop(0, n_s)
        def _(s):
            @pl.when(later)
            def _():
                for t in (2, 3):
                    @pl.when(s == t - 2)
                    def _():
                        e3(t)

                arrived(s, OWN_D, ALT_D)

            @pl.when(s == last)
            def _():
                a3(j)

            t1_tick(s, x, True)

            @pl.when(later)
            def _():
                g6b(s)

                @pl.when(s < last)
                def _():
                    g5a(s + 1)

                arrived(s, DM_O, DM_A)

            @pl.when(s == 2)
            def _():
                a2()

            t1_tick(s, me.xm)

            @pl.when(later)
            def _():
                g7(s)

                @pl.when(s < last)
                def _():
                    g5b(s + 1)

                @pl.when(s < 2)
                def _():
                    e4(s + 2)
                    g4(s + 2)

                arrived(s, DP_O, DP_A)

            @pl.when(s == last)
            def _():
                b2()

            t1_tick(s, me.xp)

            @pl.when(later)
            def _():
                @pl.when(s < last)
                def _():
                    g6a(s + 1)

                arrived(s, DF_O, DF_A)

            @pl.when(s == 1)
            def _():
                a1(j)

            t1_tick(s, me.x2)

        @pl.when(later)
        def _():
            @pl.loop(0, n_s)
            def _(t):
                for k in range(N_COPY):
                    copy(k, t).wait_send()

        @pl.when(more)
        def _():
            for i, peer in enumerate((me.to_hi, me.to_xp, me.to_xm, me.to_core)):
                signal(credit.at[i], peer)

        b3(j)

        @pl.loop(0, ah // (4 * tile))
        def _(g):
            al, bp, inv = AL[...], BP[...], INV[...]
            for u in range(4):
                at_row = pl.multiple_of((g * 4 + u) * tile, tile)
                mixed = dot_hi(W3[...], jnp.concatenate(
                    [T1[s, pl.ds((2 * z + l) * ah + at_row, tile), :]
                     for z in range(CHIPS) for s in slices for l in HALVES]))
                for t in slices:
                    for r in range(n_r):
                        i = (t * n_r + r) * tile
                        at = (t, pl.ds(at_row, tile), slice(r * bh, (r + 1) * bh))
                        now = T2[at]
                        T2[at] = (mixed[i:i + tile] - al * now - bp * TP[at]) * inv
                        TP[at] = now

        BP[...] = BE[...]

        @pl.when(j == 0)
        def _():
            load_r.wait()

        def y_tick(t, which, yy):
            PY[t, which] = dot_hi(T2[t], R[:, block(yy * bw, bw)])

        def far(t):
            y_tick(t, 0, me.y2)
            e1(t)

        far(0)

        @pl.loop(0, n_s)
        def _(t):
            @pl.when(t < last)
            def _():
                far(t + 1)

            @pl.when(t == 2)
            def _():
                e4(0)

                @pl.when(more)
                def _():
                    for i in range(credit.shape[0]):
                        pl.semaphore_wait(credit.at[i], 1)
                    g4(0)

            @pl.when(jnp.logical_and(more, t == last))
            def _():
                g5a(0)

            y_tick(t, 1, me.yp)

            @pl.when(t == last)
            def _():
                e4(1)

                @pl.when(more)
                def _():
                    g5b(0)
                    g4(1)

            y_tick(t, 2, me.ym)
            e2(t)

            for i in HALVES:
                @pl.when(t == i + 1)
                def _():
                    e3(i)

            @pl.when(jnp.logical_and(more, t == last))
            def _():
                g6a(0)

            y_tick(t, 3, col)

    for t in (2, last):
        e3(t)
    for t in (2, last):
        e4(t)
    a1(STEPS)
    a2()
    a3(STEPS)
    b2()
    b3(STEPS)

    def out_at(z):
        return T1.at[:, block(lo_of(z) * aw + hi_of(z) * ah, ah), :]

    mine = out_at(mpo)
    T1[:, block(lo * aw + hi * ah, ah), :] = V[1 - STEPS % 2]

    def spread(dz):
        return remote(mine, mine, z_s.at[dz - 1], z_r.at[dz - 1], me.turn(mpo=dz))

    for dz in FAR_FIRST:
        spread(dz).start()
    for t in slices:
        for k in range(N_REDUCE):
            copy(k, t).wait_send()
    for dz in OTHERS:
        got(out_at(lax.rem(mpo + CHIPS - dz, CHIPS)), z_s.at[dz - 1], z_r.at[dz - 1], here)
    outs = [pltpu.make_async_copy(T1.at[t, h * aw:(h + 1) * aw, :], out.at[:, t // 2, t % 2, h * bh:(h + 1) * bh],
                                  o_s.at[t, h]) for t in slices for h in HALVES]
    for part in outs:
        part.start()
    for dz in OTHERS:
        spread(dz).wait_send()
    for part in outs:
        part.wait()


def solution(mesh):
    dma = pltpu.SemaphoreType.DMA
    anywhere, vmem = (pl.BlockSpec(memory_space=m) for m in (pl.ANY, pltpu.VMEM))

    def shape(*dims):
        return jax.ShapeDtypeStruct(dims, F32)

    def keep(*dims, dtype=F32):
        return pltpu.VMEM(dims, dtype)

    def local_fn(psi_blk, left_blk, right_blk, mpo_blk):
        aw, bw, nb = psi_blk.shape[0], psi_blk.shape[-1], right_blk.shape[-1]
        ah, bh, n_l, n_s = aw // 2, bw // 2, 2 * CHIPS, CHIPS
        tile, lanes = 8, min(128, bh)
        w = mpo_blk.reshape(2, n_l, n_s, n_s).transpose(3, 1, 2, 0).reshape(n_s * n_l, n_l)
        w = jnp.pad(jnp.repeat(w, tile, axis=1), ((0, 0), (0, n_l * tile)))
        two, nine, far = dma((2,)), dma((9,)), dma((3,))
        hg, lg, rg, wg = pl.pallas_call(
            setup_kernel,
            out_shape=(shape(n_s, nb, bh), shape(n_l, ROWS, CHIPS, aw // CHIPS, ah), shape(n_l * bh, nb),
                       shape(CHIPS, *w.shape)),
            in_specs=[anywhere] * 4,
            out_specs=[anywhere] * 4,
            scratch_shapes=[
                keep(n_s, aw, bh), keep(2, bh, nb), dma((n_s, 9)), dma((n_s, 9)), dma, dma, dma((4,)), dma((4,)),
                dma((3, 2, 2)), dma((3, 2, 2)), nine, nine, dma, dma, far, far, dma((7,)),
            ],
            compiler_params=pltpu.CompilerParams(collective_id=0, has_side_effects=True),
            name='setup',
        )(psi_blk, left_blk, right_blk, w)

        lt = lg.reshape(n_l, nb, ah).transpose(0, 2, 1).reshape(n_l * ah, nb)
        v_next, ab = pl.pallas_call(
            lanczos,
            out_shape=(shape(*psi_blk.shape), shape(2, STEPS + 1, tile, lanes)),
            in_specs=[anywhere, anywhere, anywhere, vmem],
            out_specs=[anywhere, vmem],
            scratch_shapes=[
                keep(n_l * bh, nb), keep(n_l * ah, nb), keep(n_s, nb, bh), keep(n_s * n_l, 256),
                keep(256, 256), keep(n_s, n_l * ah, bh), keep(n_s, ah, n_l * bh),
                keep(n_s, ah, n_l * bh), keep(n_s, 4, ah, bw), keep(n_s, 2, ah, bh), keep(n_s, 2, ah, bw),
                keep(n_s, ah, bh), keep(2, n_s, ah, bh), *[keep(tile, bh)] * 4,
                keep(2, 2, tile, lanes), keep(2, ROWS, tile, lanes), keep(2, CHIPS * CHIPS, tile, lanes),
                dma((n_s + 1, 4)), dma((n_s, N_COPY)), dma((n_s, N_COPY)), two, two, two, two,
                pltpu.SemaphoreType.REGULAR((4,)), far, far, dma((n_s, 2)),
            ],
            compiler_params=pltpu.CompilerParams(collective_id=1, has_side_effects=True, vmem_limit_bytes=62 * MIB),
            name='lanczos',
        )(hg, lt, rg, wg)
        return ab[0, 1:, 0, 0], ab[1, 1:, 0, 0], v_next

    return jax.shard_map(
        local_fn,
        mesh=mesh,
        in_specs=(P('row', None, None, 'col'), P('row', 'mpo', None), P('col', 'mpo', None),
                  P('mpo', None, None, None, None, None)),
        out_specs=(P(), P(), P('row', None, None, 'col')),
        check_vma=False,
    )
```

time: 2640 us -> 499 us (0.19)
  waiting for transfers between devices: 1430 us -> 0 us
  blocking collectives: 673 us -> 0 us
  Pallas kernels: 0 us -> 483 us
  matrix products: 330 us -> 0 us
  local copies, waits for them, and re-layouts: 122 us -> 15.6 us
  other arithmetic: 53.6 us -> 0 us
    reduce_scatter x8 -> x0, waiting for transfers between devices: 914 us -> none  [the longest x4 593 us: apply_ham(): t_two = lax.psum_scatter(t_part, 'mpo', scatter_dimension=2, tiled=True)]
    psum x9 -> x0, blocking collectives: 571 us -> none  [global_dot(): return lax.psum(jnp.sum(left_vec * right_vec), VEC_AXES)]
    pallas_call x0 -> x2, Pallas kernels: none -> 483 us  [the longest x1 368 us: local_fn(): pl.pallas_call(lanczos, out_shape=(shape(*psi_blk.shape), shape(2, STEPS...]
    dot_general x12 -> x0, matrix products: 330 us -> none  [the longest x4 128 us: apply_ham(): jnp.einsum('cbrt,brd->ctd', t_two, right_blk, precision=PREC_HIGH, prefer...]
    all_gather x4 -> x0, waiting for transfers between devices: 272 us -> none  [apply_ham(): vec_full = lax.all_gather(vec_mat, 'row', axis=0, tiled=True)]
    psum x4 -> x0, waiting for transfers between devices: 242 us -> none  [apply_ham(): return lax.psum(y_cols, 'mpo')]
    all_to_all x1 -> x0, blocking collectives: 102 us -> none  [local_fn(): left_cols = lax.all_to_all(left_blk, 'row', 2, 0, tiled=True)]
    dot_general x8 -> x0, local copies, waits for them, and re-layouts: 100 us -> none  [the longest x4 77.8 us: apply_ham(): jnp.einsum('lcsb,lrst->cbrt', t_one, mpo_mat, precision=PREC_HIGH, prefer...]
  transfers between devices with their start and end apart: 16 -> 0, of which waited for: 16 -> 0; matrix products, arithmetic and copies ran while one was open for 1% -> 0% of each run, Pallas kernels for 0% -> 0%
where the time goes in v1:
time: 499 us
  Pallas kernels  483 us (97%)
  local copies, waits for them, and re-layouts  15.6 us (3%)
    pallas_call x1, Pallas kernels, local_fn(): pl.pallas_call(lanczos, out_shape=(shape(*psi_blk.shape), shape(2, STEPS...  368 us
    pallas_call x1, Pallas kernels, local_fn(): pl.pallas_call(setup_kernel, out_shape=(shape(n_s, nb, bh), shape(n_l, RO...  115 us

profile of v1, /device:TPU:1, one launch (start us, length us, event | category | flops | bytes accessed | tf_op | source)
XLA Modules:
  0.0 499.0 jit_solution(2594993605657164719)
XLA Ops:
  0.6 0.7 copy.12
  1.4 0.1 reshape.22
  1.4 0.1 copy.9
  1.5 0.6 pad.4.w
  2.1 115.2 %setup.1 = (f32[4,2048,256]{2,1,0:T(8,128)}, f32[8,8,4,64,128]{4,3,2,1,0:T(8,128)}, f32[2048,2048]{1,0:T(8,128)}, f32[4,32,128]{2,1,0:T(8,128)}) custom-call(f32[256,2,2,512]{3,2,1,0:T(2,128)} %psi.1, f32[256,2,2048]{2,1,0:T(2,128)} %left.1, f32[512,2,2048]{2,1,0:T(2,128)} %right.1, f32[32,128]{1,0:T(8,128)} %pad.4.w), custom_call_target="tpu_custom_call" | custom-call | tf_op jit(solution)/shard_map/setup/pallas_call | solution.py:678
  117.4 9.1 %copy.10 = f32[8,2048,128]{1,2,0:T(8,128)} copy(f32[8,2048,128]{2,1,0:T(8,128)} %bitcast.13) | data formatting | bytes 16777216 | tf_op jit(solution)/shard_map/reshape | solution.py:692
  126.5 367.5 %lanczos.1 = (f32[256,2,2,512]{3,2,1,0:T(2,128)}, f32[2,5,8,128]{3,2,1,0:T(8,128)}) custom-call(f32[4,2048,256]{2,1,0:T(8,128)} %get-tuple-element.9.hg, f32[1024,2048]{1,0:T(8,128)} %bitcast.12, f32[2048,2048]{1,0:T(8,128)} %get-tuple-element.11.rg, f32[4,32,128]{2,1,0:T(8,128)} %get-tuple-element.12.wg), custom_call_target="tpu_custom_call" | custom-call | tf_op jit(solution)/shard_map/lanczos/pallas_call | solution.py:693
  494.0 1.4 slice_reduce_fusion
  495.4 3.6 copy.14
  (1 shorter events, 0.0 us)

commit v2 on v1

--- a/solution.py
+++ b/solution.py
@@ -88,6 +88,10 @@
         for k in ks:
             self.copy(k).start()
 
+    def sent(self):
+        for k in range(len(self.moves)):
+            self.copy(k).wait_send()
+
     def got(self, *ks):
         for k in ks:
             got(self.lands[k], self.send.at[k], self.recv.at[k], self.device)
@@ -96,160 +100,9 @@
 (R_P, R_M, R_CORE, R_FWD_P, R_FWD_M, R_CORE_M, R_CORE_P, R_CORE_F0, R_CORE_F1) = range(9)
 
 
-def setup_kernel(psi, left, right, w, hg, lg, rg, wg, st_psi, st_r, psi_s, psi_r, l1_s, l1_r, ly_s, ly_r, rz_s, rz_r,
-                 rx_s, rx_r, rd_s, rd_r, w_s, w_r, loc):
-    me = Around()
-    row, col, mpo, c, o = me.row, me.col, me.mpo, me.c, me.other
-    aw, bw, nb = psi.shape[0], psi.shape[-1], right.shape[-1]
-    ah, bh, qa = aw // 2, bw // 2, aw // CHIPS
-    half, zc, xc = nb // 2, nb // CHIPS, nb // (2 * ROWS)
-    here = me.to_core
-    plane = [(dr, dz) for dz in (2, 1, 3, 0) for dr in (4, 5, 2, 3, 6, 7, 1, 0)]
-
-    bar = pltpu.get_barrier_semaphore()
-    for dr, dz in plane[:-1]:
-        signal(bar, me.turn(row=dr, mpo=dz))
-    signal(bar, me.to_yp)
-    signal(bar, me.to_ym)
-    pl.semaphore_wait(bar, len(plane) + 1)
-
-    for dr, dz in plane:
-        to = me.turn(row=dr, mpo=dz)
-        for l in HALVES:
-            src = left.at[block(col * qa, qa), l, block(to['row'] * aw + hi_of(to['mpo']) * ah, ah)]
-            dst = lg.at[mpo * 2 + l, row, col]
-            if dr or dz:
-                remote(src, dst, l1_s, l1_r, to).start()
-            else:
-                pltpu.make_async_copy(src, dst, l1_r).start()
-
-    def r_rows(q, rl):
-        return block((q * 2 + rl) * bh, bh)
-
-    def r_src(z, rl, start, n):
-        return right.at[block(lo_of(z) * bh, bh), rl, block(start, n)]
-
-    def x_cols(x, core):
-        return half + (x * CORES + core) * xc
-
-    def r_part(g):
-        return (x_cols(me.x, c), xc) if g == 0 else (c * zc, zc)
-
-    def r_copies(g):
-        for dz in FAR_FIRST:
-            to = me.turn(mpo=dz)
-            for rl in HALVES:
-                sems = rz_s.at[dz - 1, rl, g], rz_r.at[dz - 1, rl, g]
-                yield remote(r_src(to['mpo'], rl, *r_part(g)), rg.at[r_rows(CHIPS - dz, rl), block(*r_part(g))], *sems, to)
-
-    def r_got(g):
-        for dz in FAR_FIRST:
-            for rl in HALVES:
-                got(rg.at[r_rows(CHIPS - dz, rl), block(*r_part(g))], rz_s.at[dz - 1, rl, g], rz_r.at[dz - 1, rl, g], here)
-
-    def w_copy(dz):
-        return remote(w, wg.at[mpo], w_s.at[dz - 1], w_r.at[dz - 1], me.turn(mpo=dz))
-
-    for copy in r_copies(0):
-        copy.start()
-
-    def psi_at(t):
-        def at(x, core, h=None):
-            start = (x * CORES + core) * aw
-            return hg.at[t, block(start, aw) if h is None else block(start + h * ah, ah), :]
-        return at
-
-    def psi_src(t):
-        return psi.at[:, t // 2, t % 2, block(me.lo * bh, bh)]
-
-    slices = range(CHIPS)
-    psi_rings = [Ring(me, psi_at(t), psi_src(t), psi_s.at[t], psi_r.at[t]) for t in slices]
-    for ring in psi_rings:
-        ring.start(R_P, R_M, R_CORE)
-    for copy in r_copies(1):
-        copy.start()
-    for dz in OTHERS:
-        w_copy(dz).start()
-
-    own = [(w, wg.at[mpo], None)]
-    own += [(psi_src(t), psi_at(t)(me.x, c), st_psi.at[t]) for t in slices]
-    own += [(r_src(mpo, rl, 0, nb), rg.at[r_rows(0, rl), :], st_r.at[rl]) for rl in HALVES]
-    for i, (src, dst, via) in enumerate(own):
-        pltpu.make_async_copy(src, dst if via is None else via, loc.at[i]).start()
-    for i, (src, dst, via) in enumerate(own):
-        if via is not None:
-            pltpu.make_async_copy(src, via, loc.at[i]).wait()
-            pltpu.make_async_copy(via, dst, loc.at[i]).start()
-
-    ls = range(2 * CHIPS)
-
-    def l_at(y, h=None):
-        return lg.at[0:len(ls) if h is None else CHIPS, :, y] if not h else lg.at[CHIPS:len(ls), :, y]
-
-    ly_moves = [(l_at(col), me.to_yp), (l_at(col), me.to_ym), (l_at(me.ym, 0), me.to_yp), (l_at(me.yp, 1), me.to_ym)]
-    ly = [remote(ref, ref, ly_s.at[k], ly_r.at[k], d) for k, (ref, d) in enumerate(ly_moves)]
-    ly_lands = [l_at(me.ym), l_at(me.yp), l_at(me.y2, 0), l_at(me.y2, 1)]
-
-    def ly_got(k):
-        got(ly_lands[k], ly_s.at[k], ly_r.at[k], here)
-
-    got(l_at(col), l1_s, l1_r, here)
-    ly[0].start()
-    ly[1].start()
-
-    def rx_at(x, core, h=None):
-        n = 6 * bh
-        rows = pl.ds(2 * bh, n) if h is None else pl.ds(2 * bh + h * n // 2, n // 2)
-        return rg.at[rows, block(x_cols(x, core), xc)]
-
-    r_got(0)
-    rx = Ring(me, rx_at, rx_at(me.x, c), rx_s, rx_r)
-    rx.start(R_P, R_M, R_CORE)
-    for ring in psi_rings:
-        ring.got(R_P)
-        ring.start(R_FWD_P, R_CORE_M)
-        ring.got(R_M)
-        ring.start(R_FWD_M, R_CORE_P)
-    r_got(1)
-
-    def rd_at(core):
-        return rg.at[pl.ds(2 * bh, 6 * bh), block(core * zc, zc)]
-
-    rd = remote(rd_at(c), rd_at(c), rd_s, rd_r, here)
-    rd.start()
-    rx.got(R_P)
-    rx.start(R_FWD_P, R_CORE_M)
-    rx.got(R_M)
-    rx.start(R_FWD_M, R_CORE_P)
-    for k in HALVES:
-        ly_got(k)
-        ly[2 + k].start()
-    for ring in (*psi_rings, rx):
-        ring.got(R_FWD_P)
-        ring.start(R_CORE_F0)
-        ring.got(R_FWD_M)
-        ring.start(R_CORE_F1)
-    for k in HALVES:
-        ly_got(2 + k)
-
-    for ring in (*psi_rings, rx):
-        ring.got(R_CORE, R_CORE_M, R_CORE_P, R_CORE_F0, R_CORE_F1)
-    got(rd_at(o), rd_s, rd_r, here)
-    for dz in OTHERS:
-        got(wg.at[lax.rem(mpo + CHIPS - dz, CHIPS)], w_s.at[dz - 1], w_r.at[dz - 1], here)
-    for i, (src, dst, via) in enumerate(own):
-        pltpu.make_async_copy(src if via is None else via, dst, loc.at[i]).wait()
-    for ring in (*psi_rings, rx):
-        for k in range(len(ring.moves)):
-            ring.copy(k).wait_send()
-    for copy in (*ly, *r_copies(0), *r_copies(1), *(w_copy(dz) for dz in OTHERS), rd):
-        copy.wait_send()
-    for ref in (lg.at[0:len(ls) - 1, :, 0], lg.at[0, 0:ROWS - 2, 0]):
-        remote(ref, ref, l1_s, l1_r, here).wait_send()
-
-
-def lanczos(hg, lt, rg, wg, out, ab, R, L, G, U, W3, T1, T2, TP, PY, RF, RN, RZ, V, AL, BE, BP, INV, ARS, AR1,
-                 AR2, load, send, recv, ar1_s, ar1_r, ar2_s, ar2_r, credit, z_s, z_r, o_s):
+def lanczos(psi, left, right, w, out, ab, R, L, G, WG, U, W3, T1, T2, TP, PY, RF, RN, RZ, V, AL, BE, BP, INV, ARS, AR1,
+            AR2, l_s, l_r, ly_s, ly_r, psi_s, psi_r, rz_s, rz_r, rx_s, rx_r, rd_s, rd_r, w_s, w_r, local, send, recv,
+            ar1_s, ar1_r, ar2_s, ar2_r, credit, z_free, z_s, z_r, o_s):
     me = Around()
     row, col, mpo, x, c, hi, lo = me.row, me.col, me.mpo, me.x, me.c, me.hi, me.lo
     n_s, nb, bh = G.shape
@@ -260,41 +113,208 @@
     slices, tile = range(n_s), AL.shape[0]
     others = [(dc, dz) for dc in range(CHIPS) for dz in range(CHIPS) if dc or dz]
     peers = [me.turn(row=d) for d in range(1, ROWS)] + [me.turn(col=dc, mpo=dz) for dc, dz in others]
+    plane = [(dr, dz) for dz in (*FAR_FIRST, 0) for dr in (4, 5, 2, 3, 6, 7, 1, 0)]
 
     bar = pltpu.get_barrier_semaphore()
-    for peer in peers:
+    greeted = [me.turn(row=dr, mpo=dz) for dr, dz in plane[:-1]] + [me.turn(col=dc, mpo=dz) for dc, dz in others if dc]
+    for peer in greeted:
         signal(bar, peer)
-
-    def l_load(i, k):
-        j = i % n_s
-        return pltpu.make_async_copy(lt.at[pl.ds(i * ah, ah), k * bw:(k + 1) * bw], PY.at[j, k], load.at[j, k])
-
-    n_k = range(nb // bw)
-    for i in slices:
-        for k in n_k:
-            l_load(i, k).start()
-    load_g, load_r = (pltpu.make_async_copy(src, dst, load.at[n_s, i]) for i, (src, dst) in enumerate(((hg, G), (rg, R))))
-    load_g.start()
-    load_r.start()
-
-    U[...] = jnp.concatenate([wg[z][:, :U.shape[1] // CHIPS] for z in range(CHIPS)], axis=1)
+    pl.semaphore_wait(bar, len(greeted))
+
+    wide = ROWS * ah
+    q_even, q_odd = aw // CHIPS, ah // CHIPS
+
+    def l_parts(z, y, first, n):
+        def lanes(h):
+            return pl.ds(pl.multiple_of(h * wide + first, ah), n)
+
+        return (T2.at[z, block(lax.rem(y, 2) * q_even, q_even), lanes(lax.div(y, 2))],
+                TP.at[z, block(y * q_odd, q_odd), lanes(0)], TP.at[z, :, lanes(1)])
+
+    n_kinds = range(3)
+    for kind in n_kinds:
+        for dr, dz in plane:
+            to = me.turn(row=dr, mpo=dz)
+            cols = block(to['row'] * aw + hi_of(to['mpo']) * ah, ah)
+            rows = (block(col * q_even, q_even), block(col * q_odd, q_odd), pl.ds(ah, ah))[kind]
+            src = left.at[rows, min(kind, 1), cols]
+            dst = l_parts(mpo, col, row * ah, ah)[kind]
+            if dr or dz:
+                remote(src, dst, l_s.at[kind], l_r.at[kind], to).start()
+            else:
+                pltpu.make_async_copy(src, dst, l_r.at[kind]).start()
+        if kind == 1:
+            def psi_at(t):
+                def at(xx, core, h=None):
+                    first = (xx * CORES + core) * aw
+                    return G.at[t, block(first, aw) if h is None else block(first + h * ah, ah), :]
+                return at
+
+            def psi_src(t):
+                return psi.at[:, t // 2, t % 2, block(lo * bh, bh)]
+
+            psi_rings = [Ring(me, psi_at(t), psi_src(t), psi_s.at[t], psi_r.at[t]) for t in slices]
+            for ring in psi_rings:
+                ring.start(R_P, R_M, R_CORE)
+
+    half, zc, xc = nb // 2, nb // CHIPS, nb // (2 * ROWS)
+
+    def r_rows(q, rl):
+        return block((q * 2 + rl) * bh, bh)
+
+    def r_src(z, rl, first, n):
+        return right.at[block(lo_of(z) * bh, bh), rl, block(first, n)]
+
+    def x_cols(xx, core):
+        return half + (xx * CORES + core) * xc
+
+    def r_part(g):
+        return (x_cols(x, c), xc) if g == 0 else (c * zc, zc)
+
+    def r_copies(g):
+        for dz in FAR_FIRST:
+            to = me.turn(mpo=dz)
+            for rl in HALVES:
+                sems = rz_s.at[dz - 1, rl, g], rz_r.at[dz - 1, rl, g]
+                yield remote(r_src(to['mpo'], rl, *r_part(g)), R.at[r_rows(CHIPS - dz, rl), block(*r_part(g))], *sems, to)
+
+    def r_got(g):
+        for dz in FAR_FIRST:
+            for rl in HALVES:
+                got(R.at[r_rows(CHIPS - dz, rl), block(*r_part(g))], rz_s.at[dz - 1, rl, g], rz_r.at[dz - 1, rl, g], here)
+
+    def rx_at(xx, core, h=None):
+        n = (n_r - 2) * bh
+        rows = pl.ds(2 * bh, n) if h is None else pl.ds(2 * bh + h * n // 2, n // 2)
+        return R.at[rows, block(x_cols(xx, core), xc)]
+
+    rx = Ring(me, rx_at, rx_at(x, c), rx_s, rx_r)
+
+    def rd_at(core):
+        return R.at[pl.ds(2 * bh, (n_r - 2) * bh), block(core * zc, zc)]
+
+    rd = remote(rd_at(c), rd_at(c), rd_s, rd_r, here)
+
+    def w_copy(dz):
+        return remote(w, WG.at[mpo], w_s.at[dz - 1], w_r.at[dz - 1], me.turn(mpo=dz))
+
+    for dz in OTHERS:
+        w_copy(dz).start()
+    for g in HALVES:
+        for part in r_copies(g):
+            part.start()
+
+    own = [(w, WG.at[mpo])] + [(psi_src(t), psi_at(t)(x, c)) for t in slices]
+    own += [(r_src(mpo, rl, 0, nb), R.at[r_rows(0, rl), :]) for rl in HALVES]
+    own = [pltpu.make_async_copy(src, dst, local.at[i]) for i, (src, dst) in enumerate(own)]
+    for part in own:
+        part.start()
+
+    for ref in (V, BP):
+        ref[...] = jnp.zeros_like(ref)
+
+    def quarter(y, h=None):
+        zs = slice(0, CHIPS) if h is None else slice(2 * h, 2 * h + 2)
+        return [ref.at[zs] for ref in (T2.at[:, block(lax.rem(y, 2) * q_even, q_even), block(lax.div(y, 2) * wide, wide)],
+                                       TP.at[:, block(y * q_odd, q_odd), pl.ds(0, wide)])]
+
+    def ly(k):
+        refs, to = ((quarter(col), me.to_yp), (quarter(col), me.to_ym), (quarter(me.ym, 0), me.to_yp),
+                    (quarter(me.yp, 1), me.to_ym))[k]
+        return [remote(ref, ref, ly_s.at[k, i], ly_r.at[k, i], to) for i, ref in enumerate(refs)]
+
+    def ly_start(*ks):
+        for k in ks:
+            for part in ly(k):
+                part.start()
+
+    def ly_got(k):
+        refs = (quarter(me.ym), quarter(me.yp), quarter(me.y2, 0), quarter(me.y2, 1))[k]
+        for i, ref in enumerate(refs):
+            got(ref, ly_s.at[k, i], ly_r.at[k, i], here)
+
+    for kind, ref in enumerate(quarter(col)):
+        got(ref, l_s.at[kind], l_r.at[kind], here)
+    ly_start(0, 1)
+    for k in HALVES:
+        ly_got(k)
+        ly_start(k + 2)
+    for ring in psi_rings:
+        ring.got(R_P)
+        ring.start(R_FWD_P, R_CORE_M)
+        ring.got(R_M)
+        ring.start(R_FWD_M, R_CORE_P)
+    r_got(0)
+    rx.start(R_P, R_M, R_CORE)
+
+    for dz in OTHERS:
+        got(WG.at[lax.rem(mpo + CHIPS - dz, CHIPS)], w_s.at[dz - 1], w_r.at[dz - 1], here)
+    own[0].wait()
+    U[...] = jnp.concatenate([WG[z][:, :U.shape[1] // CHIPS] for z in range(CHIPS)], axis=1)
     lane, sub = (lax.broadcasted_iota(jnp.int32, (tile, U.shape[1]), i) for i in (1, 0))
     diagonal = jnp.where(lax.rem(lane, tile) == sub, 1.0, 0.0)
     for t in slices:
-        for r in range(0, n_r, 2):
-            rows = [U[pl.ds(t * n_r + lax.rem(r + i + 2 * mpo, n_r), 1), :] * diagonal for i in HALVES]
+        for r in range(n_r):
             at = (t * n_r + r) * tile
-            W3[at:at + 2 * tile] = jnp.concatenate(rows)
-    for ref in (T2, TP, V, BP):
+            W3[at:at + tile] = U[pl.ds(t * n_r + lax.rem(r + 2 * mpo, n_r), 1), :] * diagonal
+
+    for ring in psi_rings:
+        ring.got(R_FWD_P)
+        ring.start(R_CORE_F0)
+        ring.got(R_FWD_M)
+        ring.start(R_CORE_F1)
+    got(TP.at[:, :, pl.ds(wide, wide)], l_s.at[2], l_r.at[2], here)
+    for k in HALVES:
+        ly_got(k + 2)
+    for k in range(CHIPS):
+        for part in ly(k):
+            part.wait_send()
+
+    @pl.loop(0, CHIPS)
+    def _(z):
+        for l, ref in enumerate((T2, TP)):
+            for h in HALVES:
+                for rr in range(ROWS):
+                    first = h * wide + rr * ah
+                    L[block((2 * z + l) * ah, ah), rr * aw + h * ah:rr * aw + (h + 1) * ah] = ref[z, :, first:first + ah].T
+
+    for ref in (T2, TP):
         ref[...] = jnp.zeros_like(ref)
-    for i in range(n_r):
-        for k in n_k:
-            l_load(i, k).wait()
-            L[i * ah:(i + 1) * ah, k * bw:(k + 1) * bw] = PY[i % n_s, k]
-            if i < n_s:
-                l_load(i + n_s, k).start()
-    pl.semaphore_wait(bar, len(peers))
-    load_g.wait()
+    for ring in psi_rings:
+        ring.got(R_CORE, R_CORE_M, R_CORE_P, R_CORE_F0, R_CORE_F1)
+    for part in own[1:1 + n_s]:
+        part.wait()
+    for ring in psi_rings:
+        ring.sent()
+
+    def r_round():
+        rx.got(R_P)
+        rx.start(R_FWD_P, R_CORE_M)
+        rx.got(R_M)
+        rx.start(R_FWD_M, R_CORE_P)
+
+    def r_cores():
+        r_got(1)
+        rd.start()
+
+    def r_far():
+        rx.got(R_FWD_P)
+        rx.start(R_CORE_F0)
+        rx.got(R_FWD_M)
+        rx.start(R_CORE_F1)
+
+    def r_end():
+        rx.got(R_CORE, R_CORE_M, R_CORE_P, R_CORE_F0, R_CORE_F1)
+        got(rd_at(o), rd_s, rd_r, here)
+        for part in own[1 + n_s:]:
+            part.wait()
+        rx.sent()
+        for part in (*r_copies(0), *r_copies(1), *(w_copy(dz) for dz in OTHERS), rd):
+            part.wait_send()
+        for kind in n_kinds:
+            for z, n in ((slice(0, CHIPS - 1), wide), (0, wide - ah)):
+                ref = l_parts(z, col, 0, n)[kind]
+                remote(ref, ref, l_s.at[kind], l_r.at[kind], here).wait_send()
 
     def rows_of(xx, cc, hh):
         return block((xx * CORES + cc) * aw + hh * ah, ah)
@@ -389,6 +409,21 @@
         arrived(t, FWD_M)
         start(t, DF_A)
 
+    newest, oldest = STEPS % 2, 1 - STEPS % 2
+
+    def z_copy(i, t, dz):
+        src = (RZ.at[t], V.at[newest, t])[i]
+        dst = TP.at[t, :, block((i * len(OTHERS) + dz - 1) * bh, bh)]
+        return remote(src, dst, z_s.at[i, t, dz - 1], z_r.at[i, t, dz - 1], me.turn(mpo=dz))
+
+    def z_start(i, t):
+        for dz in FAR_FIRST:
+            z_copy(i, t, dz).start()
+
+    def share(t):
+        RZ[t] = G[t, own_rows, :] - BP[0:1, :] * V[oldest, t]
+        z_start(0, t)
+
     def ar_pair(k, stage):
         slots, s_sem, r_sem = ((AR1, ar1_s, ar1_r), (AR2, ar2_s, ar2_r))[stage]
         n = len(peers) - len(others) if stage == 0 else len(others)
@@ -432,7 +467,7 @@
         AL[...] = jnp.full(AL.shape, ar_end(0), F32)
         al, bp, parts = AL[0:1, :], BP[0:1, :], []
         for t in slices:
-            w = G[t, own_rows, :] - al * V[p, t] - bp * V[1 - p, t]
+            w = (G[t, own_rows, :] - bp * V[1 - p, t]) - al * V[p, t]
             V[1 - p, t] = w
             parts.append(fold(w * w))
         ar_send(1, 0, sum(parts[1:], parts[0]))
@@ -451,15 +486,15 @@
 
     @pl.loop(0, STEPS)
     def _(j):
-        later, more = j > 0, j < STEPS - 1
-
-        def t1_tick(s, xx, first=False):
+        first, later, more = j == 0, j > 0, j < STEPS - 1
+
+        def t1_tick(s, xx, new=False):
             ks = block(xx * CORES * aw, CORES * aw)
             n = n_r * ah // 2
             for m in HALVES:
                 ms = slice(m * n, (m + 1) * n)
                 d = dot_hi(L[ms, ks], G[s, ks, :])
-                if first:
+                if new:
                     T1[s, ms] = d
                 else:
                     T1[s, ms] += d
@@ -494,6 +529,11 @@
             @pl.when(s == 2)
             def _():
                 a2()
+
+            for i, event in enumerate((r_cores, r_round, r_far)):
+                @pl.when(jnp.logical_and(first, s == i + 1))
+                def _():
+                    event()
 
             t1_tick(s, me.xm)
 
@@ -564,9 +604,14 @@
 
         BP[...] = BE[...]
 
-        @pl.when(j == 0)
+        @pl.when(jnp.logical_not(more))
         def _():
-            load_r.wait()
+            for dz in OTHERS:
+                signal(z_free.at[dz - 1], me.turn(mpo=dz))
+
+        @pl.when(first)
+        def _():
+            r_end()
 
         def y_tick(t, which, yy):
             PY[t, which] = dot_hi(T2[t], R[:, block(yy * bw, bw)])
@@ -579,6 +624,15 @@
 
         @pl.loop(0, n_s)
         def _(t):
+            @pl.when(jnp.logical_and(jnp.logical_not(more), t == 0))
+            def _():
+                for dz in OTHERS:
+                    pl.semaphore_wait(z_free.at[dz - 1], 1)
+
+            @pl.when(jnp.logical_not(more))
+            def _():
+                z_start(1, t)
+
             @pl.when(t < last)
             def _():
                 far(t + 1)
@@ -593,6 +647,10 @@
                         pl.semaphore_wait(credit.at[i], 1)
                     g4(0)
 
+                @pl.when(jnp.logical_not(more))
+                def _():
+                    share(0)
+
             @pl.when(jnp.logical_and(more, t == last))
             def _():
                 g5a(0)
@@ -607,6 +665,10 @@
                 def _():
                     g5b(0)
                     g4(1)
+
+                @pl.when(jnp.logical_not(more))
+                def _():
+                    share(1)
 
             y_tick(t, 2, me.ym)
             e2(t)
@@ -626,36 +688,38 @@
         e3(t)
     for t in (2, last):
         e4(t)
+        share(t)
     a1(STEPS)
     a2()
     a3(STEPS)
     b2()
+    for t in slices:
+        for i in HALVES:
+            for dz in OTHERS:
+                got(TP.at[t, :, block((i * len(OTHERS) + dz - 1) * bh, bh)], z_s.at[i, t, dz - 1], z_r.at[i, t, dz - 1], here)
     b3(STEPS)
 
     def out_at(z):
-        return T1.at[:, block(lo_of(z) * aw + hi_of(z) * ah, ah), :]
-
-    mine = out_at(mpo)
-    T1[:, block(lo * aw + hi * ah, ah), :] = V[1 - STEPS % 2]
-
-    def spread(dz):
-        return remote(mine, mine, z_s.at[dz - 1], z_r.at[dz - 1], me.turn(mpo=dz))
-
-    for dz in FAR_FIRST:
-        spread(dz).start()
+        return block(lo_of(z) * aw + hi_of(z) * ah, ah)
+
+    al, be = AL[0:1, :], BE[0:1, :]
+    for t in slices:
+        T1[t, out_at(mpo), :] = V[oldest, t]
+        for dz in OTHERS:
+            g, v = (TP[t, :, block((i * len(OTHERS) + dz - 1) * bh, bh)] for i in HALVES)
+            T1[t, out_at(lax.rem(mpo + CHIPS - dz, CHIPS)), :] = (g - al * v) / be
+        for h in HALVES:
+            pltpu.make_async_copy(T1.at[t, h * aw:(h + 1) * aw, :], out.at[:, t // 2, t % 2, h * bh:(h + 1) * bh],
+                                  o_s.at[t, h]).start()
     for t in slices:
         for k in range(N_REDUCE):
             copy(k, t).wait_send()
-    for dz in OTHERS:
-        got(out_at(lax.rem(mpo + CHIPS - dz, CHIPS)), z_s.at[dz - 1], z_r.at[dz - 1], here)
-    outs = [pltpu.make_async_copy(T1.at[t, h * aw:(h + 1) * aw, :], out.at[:, t // 2, t % 2, h * bh:(h + 1) * bh],
-                                  o_s.at[t, h]) for t in slices for h in HALVES]
-    for part in outs:
-        part.start()
-    for dz in OTHERS:
-        spread(dz).wait_send()
-    for part in outs:
-        part.wait()
+        for i in HALVES:
+            for dz in OTHERS:
+                z_copy(i, t, dz).wait_send()
+        for h in HALVES:
+            pltpu.make_async_copy(T1.at[t, h * aw:(h + 1) * aw, :], out.at[:, t // 2, t % 2, h * bh:(h + 1) * bh],
+                                  o_s.at[t, h]).wait()
 
 
 def solution(mesh):
@@ -675,38 +739,26 @@
         w = mpo_blk.reshape(2, n_l, n_s, n_s).transpose(3, 1, 2, 0).reshape(n_s * n_l, n_l)
         w = jnp.pad(jnp.repeat(w, tile, axis=1), ((0, 0), (0, n_l * tile)))
         two, nine, far = dma((2,)), dma((9,)), dma((3,))
-        hg, lg, rg, wg = pl.pallas_call(
-            setup_kernel,
-            out_shape=(shape(n_s, nb, bh), shape(n_l, ROWS, CHIPS, aw // CHIPS, ah), shape(n_l * bh, nb),
-                       shape(CHIPS, *w.shape)),
-            in_specs=[anywhere] * 4,
-            out_specs=[anywhere] * 4,
-            scratch_shapes=[
-                keep(n_s, aw, bh), keep(2, bh, nb), dma((n_s, 9)), dma((n_s, 9)), dma, dma, dma((4,)), dma((4,)),
-                dma((3, 2, 2)), dma((3, 2, 2)), nine, nine, dma, dma, far, far, dma((7,)),
-            ],
-            compiler_params=pltpu.CompilerParams(collective_id=0, has_side_effects=True),
-            name='setup',
-        )(psi_blk, left_blk, right_blk, w)
-
-        lt = lg.reshape(n_l, nb, ah).transpose(0, 2, 1).reshape(n_l * ah, nb)
         v_next, ab = pl.pallas_call(
             lanczos,
             out_shape=(shape(*psi_blk.shape), shape(2, STEPS + 1, tile, lanes)),
-            in_specs=[anywhere, anywhere, anywhere, vmem],
+            in_specs=[anywhere] * 4,
             out_specs=[anywhere, vmem],
             scratch_shapes=[
-                keep(n_l * bh, nb), keep(n_l * ah, nb), keep(n_s, nb, bh), keep(n_s * n_l, 256),
-                keep(256, 256), keep(n_s, n_l * ah, bh), keep(n_s, ah, n_l * bh),
-                keep(n_s, ah, n_l * bh), keep(n_s, 4, ah, bw), keep(n_s, 2, ah, bh), keep(n_s, 2, ah, bw),
-                keep(n_s, ah, bh), keep(2, n_s, ah, bh), *[keep(tile, bh)] * 4,
+                keep(n_l * bh, nb), keep(n_l * ah, nb), keep(n_s, nb, bh), keep(CHIPS, *w.shape), keep(n_s * n_l, 256),
+                keep(256, 256), keep(n_s, n_l * ah, bh), keep(n_s, ah, n_l * bh), keep(n_s, ah, n_l * bh),
+                keep(n_s, 4, ah, bw), keep(n_s, 2, ah, bh), keep(n_s, 2, ah, bw), keep(n_s, ah, bh),
+                keep(2, n_s, ah, bh), *[keep(tile, bh)] * 4,
                 keep(2, 2, tile, lanes), keep(2, ROWS, tile, lanes), keep(2, CHIPS * CHIPS, tile, lanes),
-                dma((n_s + 1, 4)), dma((n_s, N_COPY)), dma((n_s, N_COPY)), two, two, two, two,
-                pltpu.SemaphoreType.REGULAR((4,)), far, far, dma((n_s, 2)),
+                far, far, dma((4, 2)), dma((4, 2)), dma((n_s, 9)), dma((n_s, 9)), dma((3, 2, 2)), dma((3, 2, 2)),
+                nine, nine, dma, dma, far, far, dma((7,)),
+                dma((n_s, N_COPY)), dma((n_s, N_COPY)), two, two, two, two,
+                pltpu.SemaphoreType.REGULAR((4,)), pltpu.SemaphoreType.REGULAR((3,)), dma((2, n_s, 3)), dma((2, n_s, 3)),
+                dma((n_s, 2)),
             ],
-            compiler_params=pltpu.CompilerParams(collective_id=1, has_side_effects=True, vmem_limit_bytes=62 * MIB),
+            compiler_params=pltpu.CompilerParams(collective_id=0, has_side_effects=True, vmem_limit_bytes=62 * MIB),
             name='lanczos',
-        )(hg, lt, rg, wg)
+        )(psi_blk, left_blk, right_blk, w)
         return ab[0, 1:, 0, 0], ab[1, 1:, 0, 0], v_next
 
     return jax.shard_map(

time: 499 us -> 458 us (0.918)
  Pallas kernels: 483 us -> 451 us
  local copies, waits for them, and re-layouts: 15.6 us -> 6.49 us
    pallas_call x1 -> x0, Pallas kernels: 115 us -> none  [local_fn(): pl.pallas_call(setup_kernel, out_shape=(shape(n_s, nb, bh), shape(n_l, RO...]
    pallas_call x1, Pallas kernels: 368 us -> 451 us  [local_fn(): pl.pallas_call(lanczos, out_shape=(shape(*psi_blk.shape), shape(2, STEPS...]
    reshape x1 -> x0, local copies, waits for them, and re-layouts: 9.12 us -> none  [local_fn(): lt = lg.reshape(n_l, nb, ah).transpose(0, 2, 1).reshape(n_l * ah, nb)]
where the time goes in v2:
time: 458 us
  Pallas kernels  451 us (98%)
  local copies, waits for them, and re-layouts  6.49 us (1%)
    pallas_call x1, Pallas kernels, local_fn(): pl.pallas_call(lanczos, out_shape=(shape(*psi_blk.shape), shape(2, STEPS...  451 us

profile of v2, /device:TPU:1, one launch (start us, length us, event | category | flops | bytes accessed | tf_op | source)
XLA Modules:
  0.0 457.8 jit_solution(17584845790464110276)
XLA Ops:
  0.6 0.7 copy.10
  1.4 0.1 reshape.16
  1.4 0.1 copy.8
  1.5 0.6 pad.4.w
  2.1 450.7 %lanczos.1 = (f32[256,2,2,512]{3,2,1,0:T(2,128)}, f32[2,5,8,128]{3,2,1,0:T(8,128)}) custom-call(f32[256,2,2,512]{3,2,1,0:T(2,128)} %psi.1, f32[256,2,2048]{2,1,0:T(2,128)} %left.1, f32[512,2,2048]{2,1,0:T(2,128)} %right.1, f32[32,128]{1,0:T(8,128)} %pad.4.w), custom_call_target="tpu_custom_call" | custom-call | tf_op jit(solution)/shard_map/lanczos/pallas_call | solution.py:742
  452.8 1.4 slice_reduce_fusion
  454.2 3.6 copy.12
  (1 shorter events, 0.0 us)

commit v3 on v2

--- a/solution.py
+++ b/solution.py
@@ -100,9 +100,9 @@
 (R_P, R_M, R_CORE, R_FWD_P, R_FWD_M, R_CORE_M, R_CORE_P, R_CORE_F0, R_CORE_F1) = range(9)
 
 
-def lanczos(psi, left, right, w, out, ab, R, L, G, WG, U, W3, T1, T2, TP, PY, RF, RN, RZ, V, AL, BE, BP, INV, ARS, AR1,
+def lanczos(psi, left, right, w, out, ab, R, L, G, WG, U, W3, T1, T2, TP, PY, RF, RN, RZ, V, WS, ZB, AL, BE, BP, INV, OLD, ARS, AR1,
             AR2, l_s, l_r, ly_s, ly_r, psi_s, psi_r, rz_s, rz_r, rx_s, rx_r, rd_s, rd_r, w_s, w_r, local, send, recv,
-            ar1_s, ar1_r, ar2_s, ar2_r, credit, z_free, z_s, z_r, o_s):
+            ar1_s, ar1_r, ar2_s, ar2_r, credit, z_s, z_r, o_s):
     me = Around()
     row, col, mpo, x, c, hi, lo = me.row, me.col, me.mpo, me.x, me.c, me.hi, me.lo
     n_s, nb, bh = G.shape
@@ -210,7 +210,7 @@
     for part in own:
         part.start()
 
-    for ref in (V, BP):
+    for ref in (V, BE, BP, INV, OLD):
         ref[...] = jnp.zeros_like(ref)
 
     def quarter(y, h=None):
@@ -380,7 +380,7 @@
 
     def e4(t):
         arrived(t, LO)
-        G[t, own_rows, :] = PY[t, 3, :, block(lo * bh, bh)] + RZ[t]
+        G[t, own_rows, :] = (PY[t, 3, :, block(lo * bh, bh)] + RZ[t]) * INV[0:1, :]
 
     def g4(t):
         start(t, HI, OWN_P, OWN_M, OWN_D)
@@ -412,16 +412,14 @@
     newest, oldest = STEPS % 2, 1 - STEPS % 2
 
     def z_copy(i, t, dz):
-        src = (RZ.at[t], V.at[newest, t])[i]
-        dst = TP.at[t, :, block((i * len(OTHERS) + dz - 1) * bh, bh)]
-        return remote(src, dst, z_s.at[i, t, dz - 1], z_r.at[i, t, dz - 1], me.turn(mpo=dz))
+        return remote((RZ, WS)[i].at[t], ZB.at[i, t, dz - 1], z_s.at[i, t, dz - 1], z_r.at[i, t, dz - 1], me.turn(mpo=dz))
 
     def z_start(i, t):
         for dz in FAR_FIRST:
             z_copy(i, t, dz).start()
 
     def share(t):
-        RZ[t] = G[t, own_rows, :] - BP[0:1, :] * V[oldest, t]
+        RZ[t] = G[t, own_rows, :] - BE[0:1, :] * V[oldest, t]
         z_start(0, t)
 
     def ar_pair(k, stage):
@@ -465,7 +463,8 @@
     def a3(j):
         p = lax.rem(j, 2)
         AL[...] = jnp.full(AL.shape, ar_end(0), F32)
-        al, bp, parts = AL[0:1, :], BP[0:1, :], []
+        ab[0, j] = AL[:, :ab.shape[-1]]
+        al, bp, parts = AL[0:1, :], BE[0:1, :], []
         for t in slices:
             w = (G[t, own_rows, :] - bp * V[1 - p, t]) - al * V[p, t]
             V[1 - p, t] = w
@@ -477,12 +476,13 @@
 
     def b3(j):
         p = lax.rem(j, 2)
+        OLD[...] = INV[...]
+        BP[...] = BE[...]
         BE[...] = jnp.sqrt(jnp.full(BE.shape, ar_end(1), F32))
         INV[...] = 1.0 / BE[...]
         for t in slices:
             V[1 - p, t] = V[1 - p, t] / BE[0:1, :]
-        for i, ref in enumerate((AL, BE)):
-            ab[i, j] = ref[:, :ab.shape[-1]]
+        ab[1, j] = BE[:, :ab.shape[-1]]
 
     @pl.loop(0, STEPS)
     def _(j):
@@ -510,10 +510,6 @@
 
                 arrived(s, OWN_D, ALT_D)
 
-            @pl.when(s == last)
-            def _():
-                a3(j)
-
             t1_tick(s, x, True)
 
             @pl.when(later)
@@ -525,10 +521,6 @@
                     g5a(s + 1)
 
                 arrived(s, DM_O, DM_A)
-
-            @pl.when(s == 2)
-            def _():
-                a2()
 
             for i, event in enumerate((r_cores, r_round, r_far)):
                 @pl.when(jnp.logical_and(first, s == i + 1))
@@ -552,9 +544,9 @@
 
                 arrived(s, DP_O, DP_A)
 
-            @pl.when(s == last)
-            def _():
-                b2()
+            @pl.when(s == 2)
+            def _():
+                a2()
 
             t1_tick(s, me.xp)
 
@@ -584,11 +576,17 @@
             for i, peer in enumerate((me.to_hi, me.to_xp, me.to_xm, me.to_core)):
                 signal(credit.at[i], peer)
 
-        b3(j)
+        a3(j)
+
+        @pl.when(jnp.logical_not(more))
+        def _():
+            for t in slices:
+                WS[t] = V[newest, t]
+                z_start(1, t)
 
         @pl.loop(0, ah // (4 * tile))
         def _(g):
-            al, bp, inv = AL[...], BP[...], INV[...]
+            al, bp = AL[...] * INV[...], BE[...] * OLD[...]
             for u in range(4):
                 at_row = pl.multiple_of((g * 4 + u) * tile, tile)
                 mixed = dot_hi(W3[...], jnp.concatenate(
@@ -599,15 +597,8 @@
                         i = (t * n_r + r) * tile
                         at = (t, pl.ds(at_row, tile), slice(r * bh, (r + 1) * bh))
                         now = T2[at]
-                        T2[at] = (mixed[i:i + tile] - al * now - bp * TP[at]) * inv
+                        T2[at] = mixed[i:i + tile] - al * now - bp * TP[at]
                         TP[at] = now
-
-        BP[...] = BE[...]
-
-        @pl.when(jnp.logical_not(more))
-        def _():
-            for dz in OTHERS:
-                signal(z_free.at[dz - 1], me.turn(mpo=dz))
 
         @pl.when(first)
         def _():
@@ -621,21 +612,17 @@
             e1(t)
 
         far(0)
+        b2()
 
         @pl.loop(0, n_s)
         def _(t):
-            @pl.when(jnp.logical_and(jnp.logical_not(more), t == 0))
-            def _():
-                for dz in OTHERS:
-                    pl.semaphore_wait(z_free.at[dz - 1], 1)
-
-            @pl.when(jnp.logical_not(more))
-            def _():
-                z_start(1, t)
-
             @pl.when(t < last)
             def _():
                 far(t + 1)
+
+            @pl.when(t == 1)
+            def _():
+                b3(j)
 
             @pl.when(t == 2)
             def _():
@@ -696,7 +683,7 @@
     for t in slices:
         for i in HALVES:
             for dz in OTHERS:
-                got(TP.at[t, :, block((i * len(OTHERS) + dz - 1) * bh, bh)], z_s.at[i, t, dz - 1], z_r.at[i, t, dz - 1], here)
+                got(ZB.at[i, t, dz - 1], z_s.at[i, t, dz - 1], z_r.at[i, t, dz - 1], here)
     b3(STEPS)
 
     def out_at(z):
@@ -706,8 +693,8 @@
     for t in slices:
         T1[t, out_at(mpo), :] = V[oldest, t]
         for dz in OTHERS:
-            g, v = (TP[t, :, block((i * len(OTHERS) + dz - 1) * bh, bh)] for i in HALVES)
-            T1[t, out_at(lax.rem(mpo + CHIPS - dz, CHIPS)), :] = (g - al * v) / be
+            v = ZB[1, t, dz - 1] / BP[0:1, :]
+            T1[t, out_at(lax.rem(mpo + CHIPS - dz, CHIPS)), :] = (ZB[0, t, dz - 1] - al * v) / be
         for h in HALVES:
             pltpu.make_async_copy(T1.at[t, h * aw:(h + 1) * aw, :], out.at[:, t // 2, t % 2, h * bh:(h + 1) * bh],
                                   o_s.at[t, h]).start()
@@ -748,12 +735,12 @@
                 keep(n_l * bh, nb), keep(n_l * ah, nb), keep(n_s, nb, bh), keep(CHIPS, *w.shape), keep(n_s * n_l, 256),
                 keep(256, 256), keep(n_s, n_l * ah, bh), keep(n_s, ah, n_l * bh), keep(n_s, ah, n_l * bh),
                 keep(n_s, 4, ah, bw), keep(n_s, 2, ah, bh), keep(n_s, 2, ah, bw), keep(n_s, ah, bh),
-                keep(2, n_s, ah, bh), *[keep(tile, bh)] * 4,
+                keep(2, n_s, ah, bh), keep(n_s, ah, bh), keep(2, n_s, 3, ah, bh), *[keep(tile, bh)] * 5,
                 keep(2, 2, tile, lanes), keep(2, ROWS, tile, lanes), keep(2, CHIPS * CHIPS, tile, lanes),
                 far, far, dma((4, 2)), dma((4, 2)), dma((n_s, 9)), dma((n_s, 9)), dma((3, 2, 2)), dma((3, 2, 2)),
                 nine, nine, dma, dma, far, far, dma((7,)),
                 dma((n_s, N_COPY)), dma((n_s, N_COPY)), two, two, two, two,
-                pltpu.SemaphoreType.REGULAR((4,)), pltpu.SemaphoreType.REGULAR((3,)), dma((2, n_s, 3)), dma((2, n_s, 3)),
+                pltpu.SemaphoreType.REGULAR((4,)), dma((2, n_s, 3)), dma((2, n_s, 3)),
                 dma((n_s, 2)),
             ],
             compiler_params=pltpu.CompilerParams(collective_id=0, has_side_effects=True, vmem_limit_bytes=62 * MIB),

time: 458 us -> 449 us (0.980)
  Pallas kernels: 451 us -> 442 us
    pallas_call x1, Pallas kernels: 451 us -> 442 us  [local_fn(): pl.pallas_call(lanczos, out_shape=(shape(*psi_blk.shape), shape(2, STEPS...]
where the time goes in v3:
time: 449 us
  Pallas kernels  442 us (98%)
  local copies, waits for them, and re-layouts  6.49 us (1%)
    pallas_call x1, Pallas kernels, local_fn(): pl.pallas_call(lanczos, out_shape=(shape(*psi_blk.shape), shape(2, STEPS...  442 us

profile of v3, /device:TPU:1, one launch (start us, length us, event | category | flops | bytes accessed | tf_op | source)
XLA Modules:
  0.0 448.9 jit_solution(10925395610109802963)
XLA Ops:
  0.6 0.7 copy.10
  1.4 0.1 reshape.16
  1.4 0.1 copy.8
  1.5 0.6 pad.4.w
  2.1 441.7 %lanczos.1 = (f32[256,2,2,512]{3,2,1,0:T(2,128)}, f32[2,5,8,128]{3,2,1,0:T(8,128)}) custom-call(f32[256,2,2,512]{3,2,1,0:T(2,128)} %psi.1, f32[256,2,2048]{2,1,0:T(2,128)} %left.1, f32[512,2,2048]{2,1,0:T(2,128)} %right.1, f32[32,128]{1,0:T(8,128)} %pad.4.w), custom_call_target="tpu_custom_call" | custom-call | tf_op jit(solution)/shard_map/lanczos/pallas_call | solution.py:729
  443.9 1.4 slice_reduce_fusion
  445.2 3.6 copy.12
  (1 shorter events, 0.0 us)

commit v4 on v3

--- a/solution.py
+++ b/solution.py
@@ -122,40 +122,36 @@
     pl.semaphore_wait(bar, len(greeted))
 
     wide = ROWS * ah
-    q_even, q_odd = aw // CHIPS, ah // CHIPS
-
-    def l_parts(z, y, first, n):
-        def lanes(h):
-            return pl.ds(pl.multiple_of(h * wide + first, ah), n)
-
-        return (T2.at[z, block(lax.rem(y, 2) * q_even, q_even), lanes(lax.div(y, 2))],
-                TP.at[z, block(y * q_odd, q_odd), lanes(0)], TP.at[z, :, lanes(1)])
-
-    n_kinds = range(3)
-    for kind in n_kinds:
+    quart, few = aw // CHIPS, ah // 2
+    near = lax.div(col, 2)
+
+    def l_part(ref, z, first, n):
+        return ref.at[z, block(lax.rem(col, 2) * quart, quart), pl.ds(pl.multiple_of(near * wide + first, ah), n)]
+
+    landing = (T2, TP)
+    for l, ref in enumerate(landing):
         for dr, dz in plane:
             to = me.turn(row=dr, mpo=dz)
-            cols = block(to['row'] * aw + hi_of(to['mpo']) * ah, ah)
-            rows = (block(col * q_even, q_even), block(col * q_odd, q_odd), pl.ds(ah, ah))[kind]
-            src = left.at[rows, min(kind, 1), cols]
-            dst = l_parts(mpo, col, row * ah, ah)[kind]
+            src = left.at[block(col * quart, quart), l, block(to['row'] * aw + hi_of(to['mpo']) * ah, ah)]
+            dst = l_part(ref, mpo, row * ah, ah)
             if dr or dz:
-                remote(src, dst, l_s.at[kind], l_r.at[kind], to).start()
+                remote(src, dst, l_s.at[l], l_r.at[l], to).start()
             else:
-                pltpu.make_async_copy(src, dst, l_r.at[kind]).start()
-        if kind == 1:
-            def psi_at(t):
-                def at(xx, core, h=None):
-                    first = (xx * CORES + core) * aw
-                    return G.at[t, block(first, aw) if h is None else block(first + h * ah, ah), :]
-                return at
-
-            def psi_src(t):
-                return psi.at[:, t // 2, t % 2, block(lo * bh, bh)]
-
-            psi_rings = [Ring(me, psi_at(t), psi_src(t), psi_s.at[t], psi_r.at[t]) for t in slices]
-            for ring in psi_rings:
-                ring.start(R_P, R_M, R_CORE)
+                pltpu.make_async_copy(src, dst, l_r.at[l]).start()
+
+    def psi_at(t, h):
+        def at(xx, core, k=None):
+            base = h * wide + (xx * CORES + core) * ah
+            return G.at[t, block(base, ah) if k is None else block(base + k * few, few), :]
+        return at
+
+    def psi_src(t, h):
+        return psi.at[h * ah:(h + 1) * ah, t // 2, t % 2, block(lo * bh, bh)]
+
+    psi_parts = [(t, h) for t in slices for h in HALVES]
+    psi_rings = [Ring(me, psi_at(*part), psi_src(*part), psi_s.at[i], psi_r.at[i]) for i, part in enumerate(psi_parts)]
+    for ring in psi_rings:
+        ring.start(R_P, R_M, R_CORE)
 
     half, zc, xc = nb // 2, nb // CHIPS, nb // (2 * ROWS)
 
@@ -204,7 +200,7 @@
         for part in r_copies(g):
             part.start()
 
-    own = [(w, WG.at[mpo])] + [(psi_src(t), psi_at(t)(x, c)) for t in slices]
+    own = [(w, WG.at[mpo])] + [(psi_src(*part), psi_at(*part)(x, c)) for part in psi_parts]
     own += [(r_src(mpo, rl, 0, nb), R.at[r_rows(0, rl), :]) for rl in HALVES]
     own = [pltpu.make_async_copy(src, dst, local.at[i]) for i, (src, dst) in enumerate(own)]
     for part in own:
@@ -215,30 +211,29 @@
 
     def quarter(y, h=None):
         zs = slice(0, CHIPS) if h is None else slice(2 * h, 2 * h + 2)
-        return [ref.at[zs] for ref in (T2.at[:, block(lax.rem(y, 2) * q_even, q_even), block(lax.div(y, 2) * wide, wide)],
-                                       TP.at[:, block(y * q_odd, q_odd), pl.ds(0, wide)])]
+        rows, lanes = block(lax.rem(y, 2) * quart, quart), block(lax.div(y, 2) * wide, wide)
+        return [ref.at[zs, rows, lanes] for ref in landing]
 
     def ly(k):
         refs, to = ((quarter(col), me.to_yp), (quarter(col), me.to_ym), (quarter(me.ym, 0), me.to_yp),
                     (quarter(me.yp, 1), me.to_ym))[k]
         return [remote(ref, ref, ly_s.at[k, i], ly_r.at[k, i], to) for i, ref in enumerate(refs)]
 
-    def ly_start(*ks):
+    def ly_got(l, *ks):
         for k in ks:
-            for part in ly(k):
-                part.start()
-
-    def ly_got(k):
-        refs = (quarter(me.ym), quarter(me.yp), quarter(me.y2, 0), quarter(me.y2, 1))[k]
-        for i, ref in enumerate(refs):
-            got(ref, ly_s.at[k, i], ly_r.at[k, i], here)
-
-    for kind, ref in enumerate(quarter(col)):
-        got(ref, l_s.at[kind], l_r.at[kind], here)
-    ly_start(0, 1)
-    for k in HALVES:
-        ly_got(k)
-        ly_start(k + 2)
+            ref = (quarter(me.ym), quarter(me.yp), quarter(me.y2, 0), quarter(me.y2, 1))[k][l]
+            got(ref, ly_s.at[k, l], ly_r.at[k, l], here)
+
+    def ly_on(l):
+        for k in HALVES:
+            ly_got(l, k)
+            ly(k + 2)[l].start()
+
+    for l in HALVES:
+        got(quarter(col)[l], l_s.at[l], l_r.at[l], here)
+        for k in HALVES:
+            ly(k)[l].start()
+    ly_on(0)
     for ring in psi_rings:
         ring.got(R_P)
         ring.start(R_FWD_P, R_CORE_M)
@@ -258,31 +253,25 @@
             at = (t * n_r + r) * tile
             W3[at:at + tile] = U[pl.ds(t * n_r + lax.rem(r + 2 * mpo, n_r), 1), :] * diagonal
 
+    ly_on(1)
     for ring in psi_rings:
         ring.got(R_FWD_P)
         ring.start(R_CORE_F0)
         ring.got(R_FWD_M)
         ring.start(R_CORE_F1)
-    got(TP.at[:, :, pl.ds(wide, wide)], l_s.at[2], l_r.at[2], here)
-    for k in HALVES:
-        ly_got(k + 2)
-    for k in range(CHIPS):
-        for part in ly(k):
-            part.wait_send()
-
-    @pl.loop(0, CHIPS)
-    def _(z):
-        for l, ref in enumerate((T2, TP)):
-            for h in HALVES:
+
+    def turn_over(h):
+        @pl.loop(0, CHIPS)
+        def _(z):
+            for l, ref in enumerate(landing):
                 for rr in range(ROWS):
-                    first = h * wide + rr * ah
-                    L[block((2 * z + l) * ah, ah), rr * aw + h * ah:rr * aw + (h + 1) * ah] = ref[z, :, first:first + ah].T
-
-    for ref in (T2, TP):
-        ref[...] = jnp.zeros_like(ref)
+                    lanes = block(h * wide + rr * ah, ah)
+                    L[block((2 * z + l) * ah, ah), lanes] = ref[z, :, lanes].T
+
+    turn_over(near)
     for ring in psi_rings:
         ring.got(R_CORE, R_CORE_M, R_CORE_P, R_CORE_F0, R_CORE_F1)
-    for part in own[1:1 + n_s]:
+    for part in own[1:1 + len(psi_parts)]:
         part.wait()
     for ring in psi_rings:
         ring.sent()
@@ -306,18 +295,18 @@
     def r_end():
         rx.got(R_CORE, R_CORE_M, R_CORE_P, R_CORE_F0, R_CORE_F1)
         got(rd_at(o), rd_s, rd_r, here)
-        for part in own[1 + n_s:]:
+        for part in own[1 + len(psi_parts):]:
             part.wait()
         rx.sent()
         for part in (*r_copies(0), *r_copies(1), *(w_copy(dz) for dz in OTHERS), rd):
             part.wait_send()
-        for kind in n_kinds:
+        for l, ref in enumerate(landing):
             for z, n in ((slice(0, CHIPS - 1), wide), (0, wide - ah)):
-                ref = l_parts(z, col, 0, n)[kind]
-                remote(ref, ref, l_s.at[kind], l_r.at[kind], here).wait_send()
+                part = l_part(ref, z, 0, n)
+                remote(part, part, l_s.at[l], l_r.at[l], here).wait_send()
 
     def rows_of(xx, cc, hh):
-        return block((xx * CORES + cc) * aw + hh * ah, ah)
+        return block(hh * wide + (xx * CORES + cc) * ah, ah)
 
     own_rows = rows_of(x, c, hi)
     low, high = slice(0, bh), slice(bh, bw)
@@ -484,65 +473,84 @@
             V[1 - p, t] = V[1 - p, t] / BE[0:1, :]
         ab[1, j] = BE[:, :ab.shape[-1]]
 
-    @pl.loop(0, STEPS)
-    def _(j):
-        first, later, more = j == 0, j > 0, j < STEPS - 1
-
-        def t1_tick(s, xx, new=False):
-            ks = block(xx * CORES * aw, CORES * aw)
-            n = n_r * ah // 2
+    def t1_half(h, new, events):
+        ks = block(h * wide, wide)
+
+        @pl.loop(0, n_s)
+        def _(s):
             for m in HALVES:
-                ms = slice(m * n, (m + 1) * n)
+                ms = slice(m * n_r * ah // 2, (m + 1) * n_r * ah // 2)
                 d = dot_hi(L[ms, ks], G[s, ks, :])
                 if new:
                     T1[s, ms] = d
                 else:
                     T1[s, ms] += d
 
-        @pl.loop(0, n_s)
-        def _(s):
-            @pl.when(later)
-            def _():
-                for t in (2, 3):
-                    @pl.when(s == t - 2)
-                    def _():
-                        e3(t)
-
-                arrived(s, OWN_D, ALT_D)
-
-            t1_tick(s, x, True)
-
-            @pl.when(later)
-            def _():
-                g6b(s)
-
-                @pl.when(s < last)
-                def _():
-                    g5a(s + 1)
-
-                arrived(s, DM_O, DM_A)
-
-            for i, event in enumerate((r_cores, r_round, r_far)):
-                @pl.when(jnp.logical_and(first, s == i + 1))
+            for when, event in events:
+                @pl.when(s == when)
                 def _():
                     event()
 
+    AL[...] = jnp.zeros_like(AL)
+    ab[0, 0] = jnp.zeros(ab.shape[2:], F32)
+    parts = []
+    for t in slices:
+        V[1, t] = G[t, own_rows, :]
+        parts.append(fold(V[1, t] * V[1, t]))
+    ar_send(1, 0, sum(parts[1:], parts[0]))
+    t1_half(near, True, ((2, r_round),))
+    for l in HALVES:
+        ly_got(l, 2, 3)
+    turn_over(1 - near)
+    t1_half(1 - near, False, ((0, r_cores), (1, r_far)))
+    for k in range(CHIPS):
+        for part in ly(k):
+            part.wait_send()
+    for ref in landing:
+        ref[...] = jnp.zeros_like(ref)
+
+    @pl.loop(0, STEPS)
+    def _(j):
+        first, later, more = j == 0, j > 0, j < STEPS - 1
+
+        def t1_tick(s, xx, new=False):
+            for m in HALVES:
+                ms = slice(m * n_r * ah // 2, (m + 1) * n_r * ah // 2)
+                ks = [block(h * wide + xx * CORES * ah, CORES * ah) for h in HALVES]
+                d = dot_hi(L[ms, ks[0]], G[s, ks[0], :]) + dot_hi(L[ms, ks[1]], G[s, ks[1], :])
+                if new:
+                    T1[s, ms] = d
+                else:
+                    T1[s, ms] += d
+
+        def t1_slice(s):
+            for t in (2, 3):
+                @pl.when(s == t - 2)
+                def _():
+                    e3(t)
+
+            arrived(s, OWN_D, ALT_D)
+            t1_tick(s, x, True)
+            g6b(s)
+
+            @pl.when(s < last)
+            def _():
+                g5a(s + 1)
+
+            arrived(s, DM_O, DM_A)
             t1_tick(s, me.xm)
-
-            @pl.when(later)
-            def _():
-                g7(s)
-
-                @pl.when(s < last)
-                def _():
-                    g5b(s + 1)
-
-                @pl.when(s < 2)
-                def _():
-                    e4(s + 2)
-                    g4(s + 2)
-
-                arrived(s, DP_O, DP_A)
+            g7(s)
+
+            @pl.when(s < last)
+            def _():
+                g5b(s + 1)
+
+            @pl.when(s < 2)
+            def _():
+                e4(s + 2)
+                g4(s + 2)
+
+            arrived(s, DP_O, DP_A)
 
             @pl.when(s == 2)
             def _():
@@ -550,19 +558,21 @@
 
             t1_tick(s, me.xp)
 
-            @pl.when(later)
-            def _():
-                @pl.when(s < last)
-                def _():
-                    g6a(s + 1)
-
-                arrived(s, DF_O, DF_A)
+            @pl.when(s < last)
+            def _():
+                g6a(s + 1)
+
+            arrived(s, DF_O, DF_A)
 
             @pl.when(s == 1)
             def _():
                 a1(j)
 
             t1_tick(s, me.x2)
+
+        @pl.when(later)
+        def _():
+            pl.loop(0, n_s)(t1_slice)
 
         @pl.when(later)
         def _():
@@ -576,7 +586,9 @@
             for i, peer in enumerate((me.to_hi, me.to_xp, me.to_xm, me.to_core)):
                 signal(credit.at[i], peer)
 
-        a3(j)
+        @pl.when(later)
+        def _():
+            a3(j)
 
         @pl.when(jnp.logical_not(more))
         def _():
@@ -737,8 +749,8 @@
                 keep(n_s, 4, ah, bw), keep(n_s, 2, ah, bh), keep(n_s, 2, ah, bw), keep(n_s, ah, bh),
                 keep(2, n_s, ah, bh), keep(n_s, ah, bh), keep(2, n_s, 3, ah, bh), *[keep(tile, bh)] * 5,
                 keep(2, 2, tile, lanes), keep(2, ROWS, tile, lanes), keep(2, CHIPS * CHIPS, tile, lanes),
-                far, far, dma((4, 2)), dma((4, 2)), dma((n_s, 9)), dma((n_s, 9)), dma((3, 2, 2)), dma((3, 2, 2)),
-                nine, nine, dma, dma, far, far, dma((7,)),
+                two, two, dma((4, 2)), dma((4, 2)), dma((n_l, 9)), dma((n_l, 9)), dma((3, 2, 2)), dma((3, 2, 2)),
+                nine, nine, dma, dma, far, far, dma((11,)),
                 dma((n_s, N_COPY)), dma((n_s, N_COPY)), two, two, two, two,
                 pltpu.SemaphoreType.REGULAR((4,)), dma((2, n_s, 3)), dma((2, n_s, 3)),
                 dma((n_s, 2)),

time: 449 us -> 435 us (0.969)
  Pallas kernels: 442 us -> 427 us
    pallas_call x1, Pallas kernels: 442 us -> 427 us  [local_fn(): pl.pallas_call(lanczos, out_shape=(shape(*psi_blk.shape), shape(2, STEPS...]
where the time goes in v4:
time: 435 us
  Pallas kernels  427 us (98%)
  local copies, waits for them, and re-layouts  6.49 us (1%)
    pallas_call x1, Pallas kernels, local_fn(): pl.pallas_call(lanczos, out_shape=(shape(*psi_blk.shape), shape(2, STEPS...  427 us

profile of v4, /device:TPU:1, one launch (start us, length us, event | category | flops | bytes accessed | tf_op | source)
XLA Modules:
  0.0 434.5 jit_solution(3843315407141895247)
XLA Ops:
  0.6 0.7 copy.10
  1.4 0.1 reshape.16
  1.4 0.1 copy.8
  1.5 0.6 pad.4.w
  2.1 427.4 %lanczos.1 = (f32[256,2,2,512]{3,2,1,0:T(2,128)}, f32[2,5,8,128]{3,2,1,0:T(8,128)}) custom-call(f32[256,2,2,512]{3,2,1,0:T(2,128)} %psi.1, f32[256,2,2048]{2,1,0:T(2,128)} %left.1, f32[512,2,2048]{2,1,0:T(2,128)} %right.1, f32[32,128]{1,0:T(8,128)} %pad.4.w), custom_call_target="tpu_custom_call" | custom-call | tf_op jit(solution)/shard_map/lanczos/pallas_call | solution.py:741
  429.5 1.4 slice_reduce_fusion
  430.9 3.6 copy.12
  (1 shorter events, 0.0 us)

commit v5 on v4

--- a/solution.py
+++ b/solution.py
@@ -260,13 +260,13 @@
         ring.got(R_FWD_M)
         ring.start(R_CORE_F1)
 
-    def turn_over(h):
+    def turn_over(h, which=HALVES):
         @pl.loop(0, CHIPS)
         def _(z):
-            for l, ref in enumerate(landing):
+            for l in which:
                 for rr in range(ROWS):
                     lanes = block(h * wide + rr * ah, ah)
-                    L[block((2 * z + l) * ah, ah), lanes] = ref[z, :, lanes].T
+                    L[block((l * CHIPS + z) * ah, ah), lanes] = landing[l][z, :, lanes].T
 
     turn_over(near)
     for ring in psi_rings:
@@ -473,12 +473,12 @@
             V[1 - p, t] = V[1 - p, t] / BE[0:1, :]
         ab[1, j] = BE[:, :ab.shape[-1]]
 
-    def t1_half(h, new, events):
+    def t1_half(h, new, events, which=HALVES):
         ks = block(h * wide, wide)
 
         @pl.loop(0, n_s)
         def _(s):
-            for m in HALVES:
+            for m in which:
                 ms = slice(m * n_r * ah // 2, (m + 1) * n_r * ah // 2)
                 d = dot_hi(L[ms, ks], G[s, ks, :])
                 if new:
@@ -499,10 +499,10 @@
         parts.append(fold(V[1, t] * V[1, t]))
     ar_send(1, 0, sum(parts[1:], parts[0]))
     t1_half(near, True, ((2, r_round),))
-    for l in HALVES:
+    for l, events in enumerate(((), ((0, r_cores), (1, r_far)))):
         ly_got(l, 2, 3)
-    turn_over(1 - near)
-    t1_half(1 - near, False, ((0, r_cores), (1, r_far)))
+        turn_over(1 - near, (l,))
+        t1_half(1 - near, False, events, (l,))
     for k in range(CHIPS):
         for part in ly(k):
             part.wait_send()
@@ -602,7 +602,7 @@
             for u in range(4):
                 at_row = pl.multiple_of((g * 4 + u) * tile, tile)
                 mixed = dot_hi(W3[...], jnp.concatenate(
-                    [T1[s, pl.ds((2 * z + l) * ah + at_row, tile), :]
+                    [T1[s, pl.ds((l * CHIPS + z) * ah + at_row, tile), :]
                      for z in range(CHIPS) for s in slices for l in HALVES]))
                 for t in slices:
                     for r in range(n_r):

time: 435 us -> 430 us (0.989)
    pallas_call x1, Pallas kernels: 427 us -> 423 us  [local_fn(): pl.pallas_call(lanczos, out_shape=(shape(*psi_blk.shape), shape(2, STEPS...]
where the time goes in v5:
time: 430 us
  Pallas kernels  423 us (98%)
  local copies, waits for them, and re-layouts  6.49 us (2%)
    pallas_call x1, Pallas kernels, local_fn(): pl.pallas_call(lanczos, out_shape=(shape(*psi_blk.shape), shape(2, STEPS...  423 us

profile of v5, /device:TPU:1, one launch (start us, length us, event | category | flops | bytes accessed | tf_op | source)
XLA Modules:
  0.0 429.9 jit_solution(3631418642540702242)
XLA Ops:
  0.6 0.7 copy.10
  1.4 0.1 reshape.16
  1.4 0.1 copy.8
  1.5 0.6 pad.4.w
  2.1 422.8 %lanczos.1 = (f32[256,2,2,512]{3,2,1,0:T(2,128)}, f32[2,5,8,128]{3,2,1,0:T(8,128)}) custom-call(f32[256,2,2,512]{3,2,1,0:T(2,128)} %psi.1, f32[256,2,2048]{2,1,0:T(2,128)} %left.1, f32[512,2,2048]{2,1,0:T(2,128)} %right.1, f32[32,128]{1,0:T(8,128)} %pad.4.w), custom_call_target="tpu_custom_call" | custom-call | tf_op jit(solution)/shard_map/lanczos/pallas_call | solution.py:741
  424.9 1.4 slice_reduce_fusion
  426.3 3.6 copy.12
  (1 shorter events, 0.0 us)
